TPU v7x, 128 devices: a whole 4x4x4 slice. The times are simulated.
128 devices in a mesh: tm: 4 (over y), vox: 32 (over z, x, core).
Axes of the slice: x: 4, y: 4, z: 4, core: 2. Of those that a mesh axis runs over, the one named last changes fastest.
Arguments:
- frames: bfloat16 [4, 500, 524288], P('tm', None, 'vox'), as said below
- decay: float32 [4, 500], P('tm'), may hold values from 0.3 to 1
- start: float32 [500, 64], replicated, may hold values from -6 to 6
- clutter_cut: int32 [4], P('tm'), may hold values from 8 to 15
- noise_cut: int32 [4], P('tm'), may hold values from 32 to 63
Outputs:
- power: float32 [4, 524288], P('tm', 'vox')
Inputs may be any that keep to these rules, and one draw needn't show every extreme that they name: `frames`: each window is a sum of temporal patterns times voxel maps, plus independent noise.
All inputs are finite; a program needn't handle non-finite values.
Results may differ from a plain program's by a relative error of at most 0.00045.
Values sent between devices are 32-bit elements; how exact they have to be, the bound alone decides.
No kernel may reach another device: no remote copies, remote signals or barrier semaphores. Data moves between devices by JAX's collectives and lax.ppermute only.
A program may use at most 128 MiB of HBM per device.

v0:
```python
import jax
import jax.numpy as jnp
from jax import lax
from jax.sharding import PartitionSpec as P

ITERS = 6


def entering(part, axis, combine, identity):
    place = lax.axis_index(axis)
    gathered = jax.tree.map(lambda a: lax.all_gather(a, axis), part)
    state = jax.tree.map(lambda a, e: jnp.zeros_like(a) + jnp.asarray(e, a.dtype), part, identity)

    def one(turn, state):
        return combine(
            state, jax.tree.map(lambda a: lax.dynamic_index_in_dim(a, turn, 0, False), gathered)
        )

    return lax.fori_loop(0, place, one, state)


def split_up(shard, dim, count):
    dims = shard.shape
    pieces = shard.reshape(*dims[:dim], count, dims[dim] // count, *dims[dim + 1 :])
    return jnp.moveaxis(pieces, dim, 0)


def sum_at_owner(shard, axis, dim):
    count = lax.axis_size(axis)
    pieces = lax.all_to_all(split_up(shard, dim, count), axis, 0, 0, tiled=True)
    return jnp.sum(pieces, axis=0)


def laid_out(pieces, dim):
    pieces = jnp.moveaxis(pieces, 0, dim)
    dims = pieces.shape
    return pieces.reshape(*dims[:dim], dims[dim] * dims[dim + 1], *dims[dim + 2 :])


def sent_to_all(shard, axis):
    copies = jnp.broadcast_to(shard, (lax.axis_size(axis), *shard.shape))
    return lax.all_to_all(copies, axis, split_axis=0, concat_axis=0, tiled=True)


def collect(shard, axis, dim):
    return laid_out(sent_to_all(shard, axis), dim)


def orthonormal(product):
    highest = lax.Precision.HIGHEST
    for sweep_index in range(2):
        cross_gram = jnp.dot(product.T, product, precision=highest)
        factor = jnp.linalg.cholesky(cross_gram)
        product = lax.linalg.triangular_solve(
            factor, product, left_side=False, lower=True, transpose_a=True
        )
    return product


def chain_steps(forget, summed, weigh):

    def combine(earlier, later):
        return (earlier[0] * later[0], weigh(later[0], earlier[1]) + later[1])

    identity = (jnp.ones_like(forget), jnp.zeros_like(summed))
    before = entering((forget, summed), "tm", combine, identity)
    return weigh(forget, before[1]) + summed


def per_device(frames, decay, start, clutter_cut, noise_cut):
    highest = lax.Precision.HIGHEST
    window = frames[0]
    forget = decay[0]
    frame_count = window.shape[0]
    group_count = lax.axis_size("vox")
    share_rows = -(-frame_count // group_count)
    padded_rows = share_rows * group_count
    extra_rows = padded_rows - frame_count
    padded = jnp.pad(window, ((0, extra_rows), (0, 0)))
    position = lax.axis_index("vox")
    summed = sum_at_owner(
        lax.dot_general(
            padded, window, (((1,), (1,)), ((), ())), preferred_element_type=jnp.float32
        ),
        "vox",
        0,
    )

    def weigh(rates, held):
        longer = jnp.pad(rates, (0, extra_rows))
        row_rates = lax.dynamic_slice_in_dim(longer, position * share_rows, share_rows, 0)
        return row_rates[:, None] * rates[None, :] * held

    folded_total = chain_steps(forget, summed, weigh)
    weighted = collect(folded_total, "vox", 0)[:frame_count]
    subspace = start
    for sweep_index in range(ITERS):
        subspace = orthonormal(jnp.dot(weighted, subspace, precision=highest))
    subspace_low = subspace.astype(jnp.bfloat16)
    project = lax.dot_general(
        subspace_low, window, (((0,), (0,)), ((), ())), preferred_element_type=jnp.float32
    )
    component = jnp.arange(subspace.shape[1], dtype=jnp.int32)
    passband = ((component >= clutter_cut[0]) & (component < noise_cut[0])).astype(jnp.float32)
    power_row = jnp.sum(passband[:, None] * project * project, axis=0) / frame_count
    return power_row[None, :]


def solution(mesh):
    placed = (P("tm", None, "vox"), P("tm", None), P(), P("tm"), P("tm"))
    return jax.shard_map(
        per_device, mesh=mesh, in_specs=placed, out_specs=P("tm", "vox"), check_vma=False
    )
```

profile of v0, /device:TPU:1, one launch (start us, length us, event | category | flops | bytes accessed | tf_op | source)
XLA Modules:
  0.0 263.9 jit_solution(1500242462328493046)
XLA Ops:
  0.0 14.1 %pad.17 = bf16[512,16384]{1,0:T(8,128)(2,1)} pad(bf16[500,16384]{1,0:T(8,128)(2,1)} %bitcast.206, bf16[]{:T(256)} %constant.89.clone.1), padding=0_12x0_0 | pad | bytes 33161218 | tf_op jit(solution)/shard_map/jit(_pad)/pad | solution.py:79
  14.1 18.1 %fusion = f32[32,16,500]{2,1,0:T(8,128)} fusion(bf16[32,16,16384]{2,1,0:T(8,128)(2,1)} %bitcast.213, bf16[1,500,16384]{2,1,0:T(8,128)(2,1)} %param.10), kind=kOutput, calls=%fused_computation.3 | convolution fusion | flops 8388608000 | bytes 34185216 | tf_op jit(solution)/shard_map/dot_general | solution.py:82
  32.1 9.4 %all-to-all-start = ((f32[32,16,500]{2,1,0:T(8,128)}), f32[32,16,500]{2,1,0:T(8,128)S(1)}, u32[]{:S(2)}, u32[]{:S(2)}) async-start(f32[32,16,500]{2,1,0:T(8,128)} %fusion), calls=%async_computation | async-start | bytes 2097152 | tf_op jit(solution)/shard_map/all_to_all | solution.py:30
  41.6 9.4 %all-gather.1 = f32[4,1,500]{2,1,0:T(1,128)S(1)} all-gather(f32[1,1,500]{2,1,0:T(1,128)S(1)} %bitcast.218), channel_id=1, replica_groups=mesh['tm'=4,'vox'=32] {'tm'}, dimensions={0}, use_global_device_ids=true | all-gather | bytes 10000 | tf_op jit(solution)/shard_map/all_gather | solution.py:11
  51.0 7.6 %all-to-all-done = f32[32,16,500]{2,1,0:T(8,128)S(1)} async-done(((f32[32,16,500]{2,1,0:T(8,128)}), f32[32,16,500]{2,1,0:T(8,128)S(1)}, u32[]{:S(2)}, u32[]{:S(2)}) %all-to-all-start) | async-done | bytes 1024032 | tf_op jit(solution)/shard_map/all_to_all | solution.py:30
  58.7 9.6 %all-gather = f32[64,500]{1,0:T(8,128)S(1)} all-gather(f32[16,500]{1,0:T(8,128)S(1)} %reduce_sum.18), channel_id=2, replica_groups=mesh['tm'=4,'vox'=32] {'tm'}, dimensions={0}, use_global_device_ids=true | all-gather | bytes 160000 | tf_op jit(solution)/shard_map/all_gather | solution.py:11
  68.4 1.1 broadcast_in_dim.8
  69.5 7.0 %all-to-all-start.1 = ((f32[32,16,500]{2,1,0:T(8,128)}), f32[32,16,500]{2,1,0:T(8,128)S(1)}, u32[]{:S(2)}, u32[]{:S(2)}) async-start(f32[32,16,500]{2,1,0:T(8,128)} %broadcast_in_dim.8), calls=%async_computation.1 | async-start | bytes 2097152 | tf_op jit(solution)/shard_map/all_to_all | solution.py:42
  77.8 15.7 %all-to-all-done.1 = f32[32,16,500]{2,1,0:T(8,128)S(1)} async-done(((f32[32,16,500]{2,1,0:T(8,128)}), f32[32,16,500]{2,1,0:T(8,128)S(1)}, u32[]{:S(2)}, u32[]{:S(2)}) %all-to-all-start.1) | async-done | bytes 1024032 | tf_op jit(solution)/shard_map/all_to_all | solution.py:42
  93.5 1.1 fusion.14
  95.0 5.8 %cholesky.194 = f32[64,64]{1,0:T(8,128)S(1)} custom-call(f32[64,64]{1,0:T(8,128)S(1)} %fusion.51), custom_call_target="Cholesky" | custom-call | tf_op jit(solution)/shard_map/jit(cholesky)/cholesky | solution.py:53
  100.8 0.6 compare_reduce_fusion.11
  101.5 0.7 fusion.16
  102.1 4.9 %custom-call.16 = f32[1,64,64]{1,2,0:T(8,128)S(1)} custom-call(f32[1,64,64]{2,1,0:T(8,128)S(1)} %fusion.16), custom_call_target="InvertDiagBlocksLowerTriangular" | custom-call | tf_op jit(solution)/shard_map/triangular_solve/custom-call.0 | solution.py:54
  107.7 5.8 %cholesky.205 = f32[64,64]{1,0:T(8,128)S(1)} custom-call(f32[64,64]{1,0:T(8,128)S(1)} %fusion.49), custom_call_target="Cholesky" | custom-call | tf_op jit(solution)/shard_map/jit(cholesky)/cholesky | solution.py:53
  113.6 0.6 compare_reduce_fusion.10
  114.3 0.7 fusion.17
  114.9 4.9 %custom-call.17 = f32[1,64,64]{1,2,0:T(8,128)S(1)} custom-call(f32[1,64,64]{2,1,0:T(8,128)S(1)} %fusion.17), custom_call_target="InvertDiagBlocksLowerTriangular" | custom-call | tf_op jit(solution)/shard_map/triangular_solve/custom-call.0 | solution.py:54
  120.2 1.1 fusion.12
  121.6 5.8 %cholesky.216 = f32[64,64]{1,0:T(8,128)S(1)} custom-call(f32[64,64]{1,0:T(8,128)S(1)} %fusion.47), custom_call_target="Cholesky" | custom-call | tf_op jit(solution)/shard_map/jit(cholesky)/cholesky | solution.py:53
  127.5 0.6 compare_reduce_fusion.9
  128.1 0.7 fusion.18
  128.8 4.9 %custom-call.18 = f32[1,64,64]{1,2,0:T(8,128)S(1)} custom-call(f32[1,64,64]{2,1,0:T(8,128)S(1)} %fusion.18), custom_call_target="InvertDiagBlocksLowerTriangular" | custom-call | tf_op jit(solution)/shard_map/triangular_solve/custom-call.0 | solution.py:54
  134.4 5.8 %cholesky.227 = f32[64,64]{1,0:T(8,128)S(1)} custom-call(f32[64,64]{1,0:T(8,128)S(1)} %fusion.45), custom_call_target="Cholesky" | custom-call | tf_op jit(solution)/shard_map/jit(cholesky)/cholesky | solution.py:53
  140.3 0.6 compare_reduce_fusion.8
  140.9 0.7 fusion.19
  141.6 4.9 %custom-call.19 = f32[1,64,64]{1,2,0:T(8,128)S(1)} custom-call(f32[1,64,64]{2,1,0:T(8,128)S(1)} %fusion.19), custom_call_target="InvertDiagBlocksLowerTriangular" | custom-call | tf_op jit(solution)/shard_map/triangular_solve/custom-call.0 | solution.py:54
  146.8 1.1 fusion.10
  148.2 6.0 %cholesky.238 = f32[64,64]{1,0:T(8,128)S(1)} custom-call(f32[64,64]{1,0:T(8,128)S(1)} %fusion.43), custom_call_target="Cholesky" | custom-call | tf_op jit(solution)/shard_map/jit(cholesky)/cholesky | solution.py:53
  154.3 0.6 compare_reduce_fusion.7
  154.9 0.7 fusion.20
  155.6 4.9 %custom-call.20 = f32[1,64,64]{1,2,0:T(8,128)S(1)} custom-call(f32[1,64,64]{2,1,0:T(8,128)S(1)} %fusion.20), custom_call_target="InvertDiagBlocksLowerTriangular" | custom-call | tf_op jit(solution)/shard_map/triangular_solve/custom-call.0 | solution.py:54
  161.2 5.8 %cholesky.249 = f32[64,64]{1,0:T(8,128)S(1)} custom-call(f32[64,64]{1,0:T(8,128)S(1)} %fusion.41), custom_call_target="Cholesky" | custom-call | tf_op jit(solution)/shard_map/jit(cholesky)/cholesky | solution.py:53
  167.1 0.6 compare_reduce_fusion.6
  167.7 0.7 fusion.21
  168.4 4.9 %custom-call.21 = f32[1,64,64]{1,2,0:T(8,128)S(1)} custom-call(f32[1,64,64]{2,1,0:T(8,128)S(1)} %fusion.21), custom_call_target="InvertDiagBlocksLowerTriangular" | custom-call | tf_op jit(solution)/shard_map/triangular_solve/custom-call.0 | solution.py:54
  173.6 1.1 fusion.8
  175.0 5.8 %cholesky.260 = f32[64,64]{1,0:T(8,128)S(1)} custom-call(f32[64,64]{1,0:T(8,128)S(1)} %fusion.39), custom_call_target="Cholesky" | custom-call | tf_op jit(solution)/shard_map/jit(cholesky)/cholesky | solution.py:53
  180.9 0.6 compare_reduce_fusion.5
  181.6 0.7 fusion.22
  182.2 4.9 %custom-call.22 = f32[1,64,64]{1,2,0:T(8,128)S(1)} custom-call(f32[1,64,64]{2,1,0:T(8,128)S(1)} %fusion.22), custom_call_target="InvertDiagBlocksLowerTriangular" | custom-call | tf_op jit(solution)/shard_map/triangular_solve/custom-call.0 | solution.py:54
  187.8 5.8 %cholesky.271 = f32[64,64]{1,0:T(8,128)S(1)} custom-call(f32[64,64]{1,0:T(8,128)S(1)} %fusion.37), custom_call_target="Cholesky" | custom-call | tf_op jit(solution)/shard_map/jit(cholesky)/cholesky | solution.py:53
  193.7 0.6 compare_reduce_fusion.4
  194.3 0.7 fusion.23
  195.0 4.9 %custom-call.23 = f32[1,64,64]{1,2,0:T(8,128)S(1)} custom-call(f32[1,64,64]{2,1,0:T(8,128)S(1)} %fusion.23), custom_call_target="InvertDiagBlocksLowerTriangular" | custom-call | tf_op jit(solution)/shard_map/triangular_solve/custom-call.0 | solution.py:54
  200.2 1.1 fusion.6
  201.7 5.8 %cholesky.282 = f32[64,64]{1,0:T(8,128)S(1)} custom-call(f32[64,64]{1,0:T(8,128)S(1)} %fusion.35), custom_call_target="Cholesky" | custom-call | tf_op jit(solution)/shard_map/jit(cholesky)/cholesky | solution.py:53
  207.6 0.6 compare_reduce_fusion.3
  208.2 0.7 fusion.24
  208.9 4.9 %custom-call.24 = f32[1,64,64]{1,2,0:T(8,128)S(1)} custom-call(f32[1,64,64]{2,1,0:T(8,128)S(1)} %fusion.24), custom_call_target="InvertDiagBlocksLowerTriangular" | custom-call | tf_op jit(solution)/shard_map/triangular_solve/custom-call.0 | solution.py:54
  214.5 6.1 %cholesky.293 = f32[64,64]{1,0:T(8,128)S(1)} custom-call(f32[64,64]{1,0:T(8,128)S(1)} %fusion.33), custom_call_target="Cholesky" | custom-call | tf_op jit(solution)/shard_map/jit(cholesky)/cholesky | solution.py:53
  220.6 0.6 compare_reduce_fusion.2
  221.2 0.7 fusion.25
  221.9 4.9 %custom-call.25 = f32[1,64,64]{1,2,0:T(8,128)S(1)} custom-call(f32[1,64,64]{2,1,0:T(8,128)S(1)} %fusion.25), custom_call_target="InvertDiagBlocksLowerTriangular" | custom-call | tf_op jit(solution)/shard_map/triangular_solve/custom-call.0 | solution.py:54
  227.1 1.1 fusion.4
  228.5 5.8 %cholesky.304 = f32[64,64]{1,0:T(8,128)S(1)} custom-call(f32[64,64]{1,0:T(8,128)S(1)} %fusion.31), custom_call_target="Cholesky" | custom-call | tf_op jit(solution)/shard_map/jit(cholesky)/cholesky | solution.py:53
  234.4 0.6 compare_reduce_fusion.1
  235.1 0.7 fusion.26
  235.7 4.9 %custom-call.26 = f32[1,64,64]{1,2,0:T(8,128)S(1)} custom-call(f32[1,64,64]{2,1,0:T(8,128)S(1)} %fusion.26), custom_call_target="InvertDiagBlocksLowerTriangular" | custom-call | tf_op jit(solution)/shard_map/triangular_solve/custom-call.0 | solution.py:54
  241.3 5.8 %cholesky.315 = f32[64,64]{1,0:T(8,128)S(1)} custom-call(f32[64,64]{1,0:T(8,128)S(1)} %fusion.29), custom_call_target="Cholesky" | custom-call | tf_op jit(solution)/shard_map/jit(cholesky)/cholesky | solution.py:53
  247.2 0.6 compare_reduce_fusion
  247.8 0.7 fusion.27
  248.5 4.9 %custom-call.27 = f32[1,64,64]{1,2,0:T(8,128)S(1)} custom-call(f32[1,64,64]{2,1,0:T(8,128)S(1)} %fusion.27), custom_call_target="InvertDiagBlocksLowerTriangular" | custom-call | tf_op jit(solution)/shard_map/triangular_solve/custom-call.0 | solution.py:54
  253.7 9.1 %fusion.2 = f32[16384]{0:T(1024)S(1)} fusion(f32[64]{0:T(128)S(1)} %and_convert_fusion, bf16[500,64]{0,1:T(8,128)(2,1)S(1)} %fusion.3, bf16[1,500,16384]{2,1,0:T(8,128)(2,1)} %param.10), kind=kOutput, calls=%fused_computation.6 | convolution fusion | flops 1051705344 | bytes 16513792 | tf_op jit(solution)/shard_map/dot_general | solution.py:100
  (72 shorter events, 9.4 us)
Async XLA Ops:
  0.0 93.5 %copy-start = (f32[500,64]{0,1:T(8,128)S(1)}, f32[500,64]{0,1:T(8,128)}, u32[]{:S(2)}) copy-start(f32[500,64]{0,1:T(8,128)} %param.12) | copy-start | bytes 384004
  14.1 27.5 %copy-start.1 = (f32[1,500]{1,0:T(1,128)S(1)}, f32[1,500]{1,0:T(1,128)}, u32[]{:S(2)}) copy-start(f32[1,500]{1,0:T(1,128)} %param.11) | copy-start | bytes 6004
  32.1 26.5 %all-to-all-start = ((f32[32,16,500]{2,1,0:T(8,128)}), f32[32,16,500]{2,1,0:T(8,128)S(1)}, u32[]{:S(2)}, u32[]{:S(2)}) async-start(f32[32,16,500]{2,1,0:T(8,128)} %fusion), calls=%async_computation | async-start | bytes 2097152 | tf_op jit(solution)/shard_map/all_to_all | solution.py:30
  69.5 24.0 %all-to-all-start.1 = ((f32[32,16,500]{2,1,0:T(8,128)}), f32[32,16,500]{2,1,0:T(8,128)S(1)}, u32[]{:S(2)}, u32[]{:S(2)}) async-start(f32[32,16,500]{2,1,0:T(8,128)} %broadcast_in_dim.8), calls=%async_computation.1 | async-start | bytes 2097152 | tf_op jit(solution)/shard_map/all_to_all | solution.py:42
where the time goes:
time: 269 us; the launch traced here: 264 us
  other arithmetic  146 us (54%)
  matrix products  40.6 us (15%)
  waiting for transfers between devices  23.3 us (9%)
  blocking collectives  19 us (7%)
  starting transfers between devices  16.5 us (6%)
  local copies, waits for them, and re-layouts  16.2 us (6%)
    another operation x36, other arithmetic, orthonormal(): factor = jnp.linalg.cholesky(cross_gram)  78.6 us
    another operation x24, other arithmetic, orthonormal(): lax.linalg.triangular_solve(factor, product, left_side=False, lower=True,...  66.6 us
    all_gather x2, blocking collectives, entering(): gathered = jax.tree.map(lambda a: lax.all_gather(a, axis), part)  19 us
    dot_general x1, matrix products, per_device(): lax.dot_general(padded, window, (((1,), (1,)), ((), ())), preferred_eleme...  18.1 us
    all_to_all x1, waiting for transfers between devices, sent_to_all(): return lax.all_to_all(copies, axis, split_axis=0, concat_axis=0, tiled=True)  15.7 us
    pad x1, local copies, waits for them, and re-layouts, per_device(): padded = jnp.pad(window, ((0, extra_rows), (0, 0)))  14.1 us
    all_to_all x1, starting transfers between devices, sum_at_owner(): pieces = lax.all_to_all(split_up(shard, dim, count), axis, 0, 0, tiled=True)  9.42 us
    dot_general x1, matrix products, per_device(): lax.dot_general(subspace_low, window, (((0,), (0,)), ((), ())), preferred...  9.07 us
  transfers between devices with their start and end apart: 2, of which 2 were waited for; matrix products, arithmetic and copies ran while one was open for 0% of the time, Pallas kernels for 0%

commit v1 on v0

v1 whole, which is shorter than its diff:
```python
import functools

import jax
import jax.numpy as jnp
from jax import lax
from jax.experimental import pallas as pl
from jax.experimental.pallas import tpu as pltpu
from jax.sharding import PartitionSpec as P

ITERS = 6
CHUNK = 2048
COLS = 1024


def chunk_copy(frames_ref, kept_ref, sems, turn):
    span = pl.ds(turn * CHUNK, CHUNK)
    return pltpu.make_async_copy(frames_ref.at[0, :, span], kept_ref.at[:, span], sems.at[turn])


def gram_kernel(chunks, frames_ref, packed_ref, kept_ref, top_ref, cross_ref, low_ref, sems):
    copy = functools.partial(chunk_copy, frames_ref, kept_ref, sems)

    for turn in range(chunks):
        copy(turn).start()
    top_ref[...] = jnp.zeros_like(top_ref)
    cross_ref[...] = jnp.zeros_like(cross_ref)
    low_ref[...] = jnp.zeros_like(low_ref)
    rows = kept_ref.shape[0]
    rest = rows - 256

    def product(a, b):
        return lax.dot_general(a, b, (((1,), (1,)), ((), ())), preferred_element_type=jnp.float32)

    def one(turn, carry):
        copy(turn).wait()
        span = pl.ds(pl.multiple_of(turn * CHUNK, CHUNK), CHUNK)
        upper = kept_ref[0:256, span]
        lower = kept_ref[256:rows, span]
        top_ref[...] += product(upper, upper)
        cross_ref[0:rest, :] += product(lower, upper)
        low_ref[0:rest, 0:rest] += product(lower, lower)
        return carry

    lax.fori_loop(0, chunks, one, 0)
    down = lax.broadcasted_iota(jnp.int32, (256, 256), 0)
    across = lax.broadcasted_iota(jnp.int32, (256, 256), 1)
    low = low_ref[...]
    folded = jnp.where(down >= across, top_ref[...], low)
    diagonal = jnp.sum(jnp.where(down == across, low, 0.0), axis=0, keepdims=True)
    cross = jnp.where(down == 255, jnp.broadcast_to(diagonal, (256, 256)), cross_ref[...])
    packed_ref[0:256, :] = folded[:, :128]
    packed_ref[256:512, :] = cross[:, :128]
    packed_ref[512:768, :] = folded[:, 128:]
    packed_ref[768:1024, :] = cross[:, 128:]


def local_gram(frames):
    rows, columns = frames.shape[1:]
    chunks = columns // CHUNK
    return pl.pallas_call(
        functools.partial(gram_kernel, chunks),
        out_shape=jax.ShapeDtypeStruct((1024, 128), jnp.float32),
        in_specs=[pl.BlockSpec(memory_space=pltpu.HBM)],
        out_specs=pl.BlockSpec(memory_space=pltpu.VMEM),
        scratch_shapes=[
            pltpu.VMEM((rows, columns), frames.dtype),
            pltpu.VMEM((256, 256), jnp.float32),
            pltpu.VMEM((256, 256), jnp.float32),
            pltpu.VMEM((256, 256), jnp.float32),
            pltpu.SemaphoreType.DMA((chunks,)),
        ],
        compiler_params=pltpu.CompilerParams(vmem_limit_bytes=56 * 2**20),
        cost_estimate=pl.CostEstimate(
            flops=2 * rows * rows * columns, bytes_accessed=2 * rows * columns, transcendentals=0
        ),
        name="local_gram",
    )(frames)


def chain_kernel(steps, group, parts_ref, rates_ref, out_ref):
    held = None
    for step in range(steps):
        part = jnp.sum(parts_ref[step * group : (step + 1) * group], axis=0)
        held = part if step == 0 else rates_ref[step] * held + part
        out_ref[step * group : (step + 1) * group] = jnp.broadcast_to(held[None], (group, 8, 128))


def chain(parts, rates):
    steps = rates.shape[0]
    return pl.pallas_call(
        functools.partial(chain_kernel, steps, parts.shape[0] // steps),
        out_shape=jax.ShapeDtypeStruct(parts.shape, parts.dtype),
        compiler_params=pltpu.CompilerParams(vmem_limit_bytes=4 * 2**20),
        name="chain",
    )(parts, rates)


def split(x):
    high = x.astype(jnp.bfloat16)
    rest = x - high.astype(jnp.float32)
    middle = rest.astype(jnp.bfloat16)
    return high, middle, (rest - middle.astype(jnp.float32)).astype(jnp.bfloat16)


def mul(a, b, along=0):
    return lax.dot_general(
        a, b, (((1,), (along,)), ((), ())), preferred_element_type=jnp.float32
    )


def full_product(left, right, along=0):
    size = left[0].shape[0]
    stacked = jnp.concatenate(left, axis=0)
    first = mul(stacked, right[0], along)
    second = mul(stacked[: 2 * size], right[1], along)
    third = mul(left[0], right[2], along)
    small = first[2 * size :] + second[size:] + third
    return first[:size] + (first[size : 2 * size] + second[:size] + small)


def spread(x, index):
    return jnp.broadcast_to(x[index : index + 1, :], x.shape)


def eliminated(rows):
    rows = list(rows)
    count = len(rows)
    sub = lax.broadcasted_iota(jnp.int32, (8, 128), 0)
    scales = []
    for block in range(count):
        columns = {
            v: [
                jnp.broadcast_to(rows[v][:, 8 * block + k : 8 * block + k + 1], (8, 128))
                for k in range(8)
            ]
            for v in range(block, count)
        }
        pivots = jnp.ones((8, 128), jnp.float32)
        for j in range(8):
            pivot = spread(columns[block][j], j)
            pivots = jnp.where(sub == j, pivot, pivots)
            inverse = 1.0 / pivot
            row = spread(rows[block], j) * inverse
            parts = {k: spread(columns[block][k], j) * inverse for k in range(j + 1, 8)}
            for v in range(block, count):
                lead = columns[v][j]
                if v == block:
                    lead = jnp.where(sub > j, lead, 0.0)
                for k in range(j + 1, 8):
                    columns[v][k] = columns[v][k] - lead * parts[k]
                rows[v] = rows[v] - lead * row
        scales.append(lax.rsqrt(pivots))
    return [r * s for r, s in zip(rows, scales)]


def power_kernel(
    chunks, packed_ref, start_ref, low_ref, high_ref, frames_ref, out_ref,
    a1_ref, a2_ref, a3_ref, kept_ref, sems,
):
    copy = functools.partial(chunk_copy, frames_ref, kept_ref, sems)
    for turn in range(chunks):
        copy(turn).start()
    down = lax.broadcasted_iota(jnp.int32, (256, 256), 0)
    across = lax.broadcasted_iota(jnp.int32, (256, 256), 1)
    folded = jnp.concatenate([packed_ref[0:256, :], packed_ref[512:768, :]], axis=1)
    cross = jnp.concatenate([packed_ref[256:512, :], packed_ref[768:1024, :]], axis=1)
    turned = folded.T
    top = jnp.where(down >= across, folded, turned)
    low = jnp.where(down < across, folded, turned)
    low = jnp.where(down == across, jnp.broadcast_to(cross[255:256, :], (256, 256)), low)
    cross = jnp.where(down == 255, 0.0, cross)

    def put(piece, i, j):
        for ref, part in zip((a1_ref, a2_ref, a3_ref), split(piece)):
            ref[256 * i : 256 * (i + 1), 256 * j : 256 * (j + 1)] = part

    put(top, 0, 0)
    put(low, 1, 1)
    put(cross, 1, 0)
    put(cross.T, 0, 1)

    rank, frames = start_ref.shape
    beside = lax.broadcasted_iota(jnp.int32, (rank, 128), 0) + rank
    unit = jnp.where(
        lax.broadcasted_iota(jnp.int32, (rank, 128), 1) == beside, 1.0, 0.0
    ).astype(jnp.float32)
    none = jnp.zeros((rank, frames), jnp.bfloat16)

    def sweep(turn, product):
        parts = split(product)
        right = [jnp.concatenate([p, none], axis=0) for p in parts]
        grown = full_product(parts, right, 1) + unit
        rows = eliminated([grown[8 * v : 8 * (v + 1), :] for v in range(rank // 8)])
        factor = jnp.concatenate(rows, axis=0)
        return full_product(split(factor), [jnp.concatenate([none, p], axis=0) for p in parts])

    def iteration(turn, subspace):
        product = full_product(split(subspace), (a1_ref[...], a2_ref[...], a3_ref[...]))
        return lax.fori_loop(0, 2, sweep, product)

    subspace = lax.fori_loop(0, ITERS, iteration, start_ref[...])
    rows = kept_ref.shape[0]
    subspace_low = subspace.astype(jnp.bfloat16)[:, :rows]
    component = lax.broadcasted_iota(jnp.int32, (rank, COLS), 0)
    band = (component >= low_ref[0]) & (component < high_ref[0])

    def arrive(turn, carry):
        copy(turn).wait()
        return carry

    lax.fori_loop(0, chunks, arrive, 0)

    def project(turn, carry):
        span = pl.ds(pl.multiple_of(turn * COLS, COLS), COLS)
        values = mul(subspace_low, kept_ref[:, span])
        values = jnp.where(band, values, 0.0)
        out_ref[:, span] = jnp.sum(values * values, axis=0, keepdims=True) / rows
        return carry

    lax.fori_loop(0, kept_ref.shape[1] // COLS, project, 0)


def power_of(packed, start, low, high, frames):
    rows, columns = frames.shape[1:]
    chunks = columns // CHUNK
    return pl.pallas_call(
        functools.partial(power_kernel, chunks),
        out_shape=jax.ShapeDtypeStruct((1, columns), jnp.float32),
        in_specs=[
            pl.BlockSpec(memory_space=pltpu.VMEM),
            pl.BlockSpec(memory_space=pltpu.VMEM),
            pl.BlockSpec(memory_space=pltpu.SMEM),
            pl.BlockSpec(memory_space=pltpu.SMEM),
            pl.BlockSpec(memory_space=pltpu.HBM),
        ],
        out_specs=pl.BlockSpec(memory_space=pltpu.VMEM),
        scratch_shapes=[pltpu.VMEM((512, 512), jnp.bfloat16)] * 3
        + [pltpu.VMEM((rows, columns), frames.dtype), pltpu.SemaphoreType.DMA((chunks,))],
        compiler_params=pltpu.CompilerParams(vmem_limit_bytes=56 * 2**20),
        name="power",
    )(packed, start, low, high, frames)


def tile_rates(decay):
    steps, group = lax.axis_size("tm"), lax.axis_size("vox")
    step = lax.axis_index("tm")
    turns = [decay] + [
        lax.ppermute(decay, "tm", [(i, (i + k) % steps) for i in range(steps)])
        for k in range(1, steps)
    ]
    every = []
    for t in range(steps):
        mine = jnp.zeros_like(decay)
        for k in range(steps):
            mine = mine + jnp.where((step - t) % steps == k, turns[k], 0.0)
        every.append(mine)
    rates = jnp.stack(every)
    rates = jnp.pad(rates, ((0, 0), (0, 512 - rates.shape[1])))
    tile = step * group + lax.axis_index("vox")
    first_row = 8 * (tile % 64)
    first_column = 128 * (tile // 64)
    row = first_row + lax.broadcasted_iota(jnp.int32, (8, 128), 0)
    column = first_column + lax.broadcasted_iota(jnp.int32, (8, 128), 1)

    def at_rows(first):
        return lax.dynamic_slice_in_dim(rates, first, 8, 1)[:, :, None]

    def at_columns(first):
        return lax.dynamic_slice_in_dim(rates, first, 128, 1)[:, None, :]

    upper = at_rows(first_row) * at_columns(first_column)
    last = at_columns(256 + first_column)
    lower = at_rows(jnp.minimum(256 + first_row, 504)) * last
    return jnp.where(
        row == 511,
        last * last,
        jnp.where((row >= 256) | (row >= column), upper, lower),
    )


def per_device(frames, decay, start, clutter_cut, noise_cut):
    rates = tile_rates(decay[0])
    packed = local_gram(frames)
    parts = lax.all_to_all(packed.reshape(128, 8, 128), ("tm", "vox"), 0, 0, tiled=True)
    held = lax.all_to_all(chain(parts, rates), ("tm", "vox"), 0, 0, tiled=True)
    begin = jnp.pad(start.T, ((0, 0), (0, 512 - start.shape[0])))
    return power_of(held.reshape(1024, 128), begin, clutter_cut, noise_cut, frames)


def solution(mesh):
    placed = (P("tm", None, "vox"), P("tm", None), P(), P("tm"), P("tm"))
    return jax.shard_map(
        per_device, mesh=mesh, in_specs=placed, out_specs=P("tm", "vox"), check_vma=False
    )
```

time: 269 us -> 95.6 us (0.36); the launches traced: 264 us -> 95.3 us
  other arithmetic: 146 us -> 0.22 us
  Pallas kernels: 0 us -> 47.5 us
  matrix products: 40.6 us -> 0 us
  blocking collectives: 19 us -> 0 us
  local copies, waits for them, and re-layouts: 16.2 us -> 1.56 us
  starting transfers between devices: 16.5 us -> 19.8 us
    another operation x60 -> x1, other arithmetic: 145 us -> 0.02 us  [tile_rates(): rates = jnp.stack(every)]
    pallas_call x0 -> x3, Pallas kernels: none -> 47.5 us  [the longest x1 36 us: power_of(): pl.pallas_call(functools.partial(power_kernel, chunks), out_shape=jax.Sha...]
    dot_general x20 -> x0, matrix products: 36.6 us -> none  [the longest x1 18.1 us: per_device(): lax.dot_general(padded, window, (((1,), (1,)), ((), ())), preferred_eleme...]
    all_gather x2 -> x0, blocking collectives: 19 us -> none  [entering(): gathered = jax.tree.map(lambda a: lax.all_gather(a, axis), part)]
    pad x1, local copies, waits for them, and re-layouts: 14.1 us -> 0.66 us  [per_device(): begin = jnp.pad(start.T, ((0, 0), (0, 512 - start.shape[0])))]
    ppermute x0 -> x3, starting transfers between devices: none -> 4.59 us  [tile_rates(): lax.ppermute(decay, 'tm', [(i, (i + k) % steps) for i in range(steps)])]
    another operation x12 -> x0, matrix products: 4.03 us -> none  [orthonormal(): lax.linalg.triangular_solve(factor, product, left_side=False, lower=True,...]
  transfers between devices with their start and end apart: 2 -> 5, of which waited for: 2 -> 2; matrix products, arithmetic and copies ran while one was open for 0% -> 1% of each run, Pallas kernels for 0% -> 11%
where the time goes in v1:
time: 95.6 us; the launch traced here: 95.3 us
  Pallas kernels  47.5 us (50%)
  waiting for transfers between devices  24.8 us (26%)
  starting transfers between devices  19.8 us (21%)
  local copies, waits for them, and re-layouts  1.56 us (2%)
  between operations  1.52 us (2%)
    pallas_call x1, Pallas kernels, power_of(): pl.pallas_call(functools.partial(power_kernel, chunks), out_shape=jax.Sha...  36 us
    all_to_all x1, waiting for transfers between devices, per_device(): lax.all_to_all(packed.reshape(128, 8, 128), ('tm', 'vox'), 0, 0, tiled=True)  13.1 us
    all_to_all x1, waiting for transfers between devices, per_device(): held = lax.all_to_all(chain(parts, rates), ('tm', 'vox'), 0, 0, tiled=True)  11.6 us
    pallas_call x1, Pallas kernels, local_gram(): pl.pallas_call(functools.partial(gram_kernel, chunks), out_shape=jax.Shap...  10.6 us
    all_to_all x1, starting transfers between devices, per_device(): lax.all_to_all(packed.reshape(128, 8, 128), ('tm', 'vox'), 0, 0, tiled=True)  10.6 us
    all_to_all x1, starting transfers between devices, per_device(): held = lax.all_to_all(chain(parts, rates), ('tm', 'vox'), 0, 0, tiled=True)  4.6 us
    ppermute x3, starting transfers between devices, tile_rates(): lax.ppermute(decay, 'tm', [(i, (i + k) % steps) for i in range(steps)])  4.59 us
  transfers between devices with their start and end apart: 5, of which 2 were waited for; matrix products, arithmetic and copies ran while one was open for 1% of the time, Pallas kernels for 11%

profile of v1, /device:TPU:1, one launch (start us, length us, event | category | flops | bytes accessed | tf_op | source)
XLA Modules:
  0.0 95.3 jit_solution(15876695568901830425)
XLA Ops:
  0.0 0.0 copy-start.2
  0.0 0.0 copy-start.1
  0.0 3.6 %collective-permute-start.2 = (f32[500]{0:T(512)}, f32[500]{0:T(512)S(1)}, u32[]{:S(2)}, u32[]{:S(2)}) collective-permute-start(f32[500]{0:T(512)} %bitcast.11), channel_id=1, source_target_pairs={{0,96},{32,0},{64,32},{96,64},{1,97},{33,1},{65,33},{97,65},{2,98}... | collective-permute-start | bytes 6008 | tf_op jit(solution)/shard_map/ppermute | solution.py:248
  3.6 0.3 collective-permute-start.1
  3.9 0.7 collective-permute-start
  4.6 10.6 %local_gram.1 = f32[1024,128]{1,0:T(8,128)} custom-call(bf16[1,500,16384]{2,1,0:T(8,128)(2,1)} %frames_ref.3), custom_call_target="tpu_custom_call" | custom-call | flops 8192000000 | bytes 16384000 | tf_op jit(solution)/shard_map/local_gram/pallas_call | solution.py:60
  15.3 10.6 %all-to-all-start = ((f32[128,8,128]{2,1,0:T(8,128)}), f32[128,8,128]{2,1,0:T(8,128)S(1)}, u32[]{:S(2)}, u32[]{:S(2)}) async-start(f32[128,8,128]{2,1,0:T(8,128)} %bitcast.9), calls=%async_computation | async-start | bytes 1048576 | tf_op jit(solution)/shard_map/all_to_all | solution.py:284
  26.0 0.1 compare_or_fusion
  26.1 0.0 collective-permute-done.2
  26.1 0.0 collective-permute-done.1
  26.1 0.0 collective-permute-done
  26.1 0.0 copy-done.2
  26.2 0.1 constant_dynamic-slice_fusion.2
  26.3 0.1 select_select_fusion.rates_ref
  26.3 13.1 %all-to-all-done.parts_ref = f32[128,8,128]{2,1,0:T(8,128)S(1)} async-done(((f32[128,8,128]{2,1,0:T(8,128)}), f32[128,8,128]{2,1,0:T(8,128)S(1)}, u32[]{:S(2)}, u32[]{:S(2)}) %all-to-all-start) | async-done | bytes 524320 | tf_op jit(solution)/shard_map/all_to_all | solution.py:284
  39.5 0.9 chain.1
  40.3 4.6 %all-to-all-start.1 = ((f32[128,8,128]{2,1,0:T(8,128)}), f32[128,8,128]{2,1,0:T(8,128)S(1)}, u32[]{:S(2)}, u32[]{:S(2)}) async-start(f32[128,8,128]{2,1,0:T(8,128)} %chain.1), calls=%async_computation.1 | async-start | bytes 1048576 | tf_op jit(solution)/shard_map/all_to_all | solution.py:285
  46.2 0.0 copy-done.1
  46.2 0.7 pad.9.start_ref
  46.9 11.6 %all-to-all-done.1 = f32[128,8,128]{2,1,0:T(8,128)S(1)} async-done(((f32[128,8,128]{2,1,0:T(8,128)}), f32[128,8,128]{2,1,0:T(8,128)S(1)}, u32[]{:S(2)}, u32[]{:S(2)}) %all-to-all-start.1) | async-done | bytes 524320 | tf_op jit(solution)/shard_map/all_to_all | solution.py:285
  58.5 0.0 copy-start
  58.5 0.8 copy-done
  59.3 36.0 %power.1 = f32[1,16384]{1,0:T(1,128)} custom-call(f32[1024,128]{1,0:T(8,128)} %bitcast.8, f32[64,512]{1,0:T(8,128)} %pad.9.start_ref, s32[1]{0:T(128)S(6)} %copy.6.low_ref, s32[1]{0:T(128)S(6)} %copy.7.high_ref, bf16[1,500,16384]{2,1,0:T(8,128)(2,1)} %frames_ref.3), custom_call_target="tpu_custom_call" | custom-call | tf_op jit(solution)/shard_map/power/pallas_call | solution.py:226
  (8 shorter events, 0.1 us)
Async XLA Ops:
  0.0 26.1 %copy-start.2 = (f32[1,500]{1,0:T(1,128)S(1)}, f32[1,500]{1,0:T(1,128)}, u32[]{:S(2)}) copy-start(f32[1,500]{1,0:T(1,128)} %param.6) | copy-start | bytes 6004
  0.0 46.2 %copy-start.1 = (f32[500,64]{0,1:T(8,128)S(1)}, f32[500,64]{0,1:T(8,128)}, u32[]{:S(2)}) copy-start(f32[500,64]{0,1:T(8,128)} %param.7) | copy-start | bytes 384004
  0.0 26.1 %collective-permute-start.2 = (f32[500]{0:T(512)}, f32[500]{0:T(512)S(1)}, u32[]{:S(2)}, u32[]{:S(2)}) collective-permute-start(f32[500]{0:T(512)} %bitcast.11), channel_id=1, source_target_pairs={{0,96},{32,0},{64,32},{96,64},{1,97},{33,1},{65,33},{97,65},{2,98}... | collective-permute-start | bytes 6008 | tf_op jit(solution)/shard_map/ppermute | solution.py:248
  3.6 22.5 %collective-permute-start.1 = (f32[500]{0:T(512)}, f32[500]{0:T(512)S(1)}, u32[]{:S(2)}, u32[]{:S(2)}) collective-permute-start(f32[500]{0:T(512)} %bitcast.12), channel_id=1, source_target_pairs={{0,64},{32,96},{64,0},{96,32},{1,65},{33,97},{65,1},{97,33},{2,66}... | collective-permute-start | bytes 6008 | tf_op jit(solution)/shard_map/ppermute | solution.py:248
  3.9 22.2 %collective-permute-start = (f32[500]{0:T(512)}, f32[500]{0:T(512)S(1)}, u32[]{:S(2)}, u32[]{:S(2)}) collective-permute-start(f32[500]{0:T(512)} %bitcast.13), channel_id=1, source_target_pairs={{0,32},{32,64},{64,96},{96,0},{1,33},{33,65},{65,97},{97,1},{2,34}... | collective-permute-start | bytes 6008 | tf_op jit(solution)/shard_map/ppermute | solution.py:248
  15.3 24.2 %all-to-all-start = ((f32[128,8,128]{2,1,0:T(8,128)}), f32[128,8,128]{2,1,0:T(8,128)S(1)}, u32[]{:S(2)}, u32[]{:S(2)}) async-start(f32[128,8,128]{2,1,0:T(8,128)} %bitcast.9), calls=%async_computation | async-start | bytes 1048576 | tf_op jit(solution)/shard_map/all_to_all | solution.py:284
  40.3 18.2 %all-to-all-start.1 = ((f32[128,8,128]{2,1,0:T(8,128)}), f32[128,8,128]{2,1,0:T(8,128)S(1)}, u32[]{:S(2)}, u32[]{:S(2)}) async-start(f32[128,8,128]{2,1,0:T(8,128)} %chain.1), calls=%async_computation.1 | async-start | bytes 1048576 | tf_op jit(solution)/shard_map/all_to_all | solution.py:285
  58.5 0.8 copy-start

commit v2 on v1

--- a/solution.py
+++ b/solution.py
@@ -5,11 +5,12 @@
 from jax import lax
 from jax.experimental import pallas as pl
 from jax.experimental.pallas import tpu as pltpu
-from jax.sharding import PartitionSpec as P
+from jax.sharding import Mesh, PartitionSpec as P
+
 
 ITERS = 6
 CHUNK = 2048
-COLS = 1024
+COLS = 4096
 
 
 def chunk_copy(frames_ref, kept_ref, sems, turn):
@@ -17,7 +18,7 @@
     return pltpu.make_async_copy(frames_ref.at[0, :, span], kept_ref.at[:, span], sems.at[turn])
 
 
-def gram_kernel(chunks, frames_ref, packed_ref, kept_ref, top_ref, cross_ref, low_ref, sems):
+def gram_kernel(chunks, core_ref, frames_ref, own_ref, other_ref, kept_ref, top_ref, cross_ref, low_ref, sems):
     copy = functools.partial(chunk_copy, frames_ref, kept_ref, sems)
 
     for turn in range(chunks):
@@ -48,20 +49,21 @@
     folded = jnp.where(down >= across, top_ref[...], low)
     diagonal = jnp.sum(jnp.where(down == across, low, 0.0), axis=0, keepdims=True)
     cross = jnp.where(down == 255, jnp.broadcast_to(diagonal, (256, 256)), cross_ref[...])
-    packed_ref[0:256, :] = folded[:, :128]
-    packed_ref[256:512, :] = cross[:, :128]
-    packed_ref[512:768, :] = folded[:, 128:]
-    packed_ref[768:1024, :] = cross[:, 128:]
-
-
-def local_gram(frames):
+    first = core_ref[0] == 0
+    for spot, piece in ((0, folded), (256, cross)):
+        left, right = piece[:, :128], piece[:, 128:]
+        own_ref[spot : spot + 256, :] = jnp.where(first, left, right)
+        other_ref[spot : spot + 256, :] = jnp.where(first, right, left)
+
+
+def local_gram(core, frames):
     rows, columns = frames.shape[1:]
     chunks = columns // CHUNK
     return pl.pallas_call(
         functools.partial(gram_kernel, chunks),
-        out_shape=jax.ShapeDtypeStruct((1024, 128), jnp.float32),
-        in_specs=[pl.BlockSpec(memory_space=pltpu.HBM)],
-        out_specs=pl.BlockSpec(memory_space=pltpu.VMEM),
+        out_shape=[pltpu.VMEM((512, 128), jnp.float32)] * 2,
+        in_specs=[pl.BlockSpec(memory_space=pltpu.SMEM), pl.BlockSpec(memory_space=pltpu.HBM)],
+        out_specs=[pl.BlockSpec(memory_space=pltpu.VMEM)] * 2,
         scratch_shapes=[
             pltpu.VMEM((rows, columns), frames.dtype),
             pltpu.VMEM((256, 256), jnp.float32),
@@ -74,7 +76,7 @@
             flops=2 * rows * rows * columns, bytes_accessed=2 * rows * columns, transcendentals=0
         ),
         name="local_gram",
-    )(frames)
+    )(core, frames)
 
 
 def chain_kernel(steps, group, parts_ref, rates_ref, out_ref):
@@ -122,48 +124,94 @@
     return jnp.broadcast_to(x[index : index + 1, :], x.shape)
 
 
-def eliminated(rows):
+def eliminated(rows, none):
     rows = list(rows)
     count = len(rows)
     sub = lax.broadcasted_iota(jnp.int32, (8, 128), 0)
-    scales = []
-    for block in range(count):
-        columns = {
-            v: [
-                jnp.broadcast_to(rows[v][:, 8 * block + k : 8 * block + k + 1], (8, 128))
-                for k in range(8)
-            ]
-            for v in range(block, count)
-        }
-        pivots = jnp.ones((8, 128), jnp.float32)
-        for j in range(8):
-            pivot = spread(columns[block][j], j)
-            pivots = jnp.where(sub == j, pivot, pivots)
-            inverse = 1.0 / pivot
-            row = spread(rows[block], j) * inverse
-            parts = {k: spread(columns[block][k], j) * inverse for k in range(j + 1, 8)}
-            for v in range(block, count):
-                lead = columns[v][j]
-                if v == block:
-                    lead = jnp.where(sub > j, lead, 0.0)
+
+    def columns_of(v, first, size):
+        return [
+            jnp.broadcast_to(rows[v][:, first + k : first + k + 1], (8, 128))
+            for k in range(size)
+        ]
+
+    done = []
+    for a in range(0, count, 2):
+        b = a + 1
+        top = [column + none for column in columns_of(a, 8 * a, 8)]
+        side = [column + none for column in columns_of(b, 8 * a, 8)]
+        low = columns_of(b, 8 * b, 8)
+        rest = {v: columns_of(v, 8 * a, 16) for v in range(b + 1, min(b + 3, count))}
+        scales = []
+        for half, own in ((0, top), (1, low)):
+            pivots = jnp.ones((8, 128), jnp.float32)
+            pivot = spread(own[0], 0)
+            for j in range(8):
+                pivots = jnp.where(sub == j, pivot, pivots)
+                inverse = 1.0 / pivot
+                heads = [spread(own[k], j) if k > j else None for k in range(8)]
+                if j < 7:
+                    pivot = spread(own[j + 1], j + 1) - (
+                        spread(own[j], j + 1) * inverse
+                    ) * heads[j + 1]
+                lead = jnp.where(sub > j, own[j], 0.0) * inverse
+                row = spread(rows[a + half], j)
+                if half == 0:
+                    beside = side[j] * inverse
+                    others = [spread(side[j], k) for k in range(8)]
+                    rows[b] = rows[b] - beside * row
+                    for k in range(8):
+                        low[k] = low[k] - beside * others[k]
+                rows[a + half] = rows[a + half] - lead * row
                 for k in range(j + 1, 8):
-                    columns[v][k] = columns[v][k] - lead * parts[k]
-                rows[v] = rows[v] - lead * row
-        scales.append(lax.rsqrt(pivots))
-    return [r * s for r, s in zip(rows, scales)]
+                    own[k] = own[k] - lead * heads[k]
+                    if half == 0:
+                        side[k] = side[k] - beside * heads[k]
+                for v, held in rest.items():
+                    far = held[8 * half + j] * inverse
+                    for k in range(j + 1, 8):
+                        held[8 * half + k] = held[8 * half + k] - far * heads[k]
+                    if half == 0:
+                        for k in range(8):
+                            held[8 + k] = held[8 + k] - far * others[k]
+                    rows[v] = rows[v] - far * row
+            scales.append(1.0 / pivots)
+            done.append(lax.rsqrt(pivots))
+        if b + 3 < count:
+            u1, u2, u3 = split(jnp.concatenate([rows[a], rows[b]], axis=0))
+            t1, t2, t3 = split(
+                jnp.concatenate([rows[a] * scales[0], rows[b] * scales[1]], axis=0)
+            )
+            change = lax.dot_general(
+                jnp.concatenate([u1, u1, u2, u2, u1, u3], axis=0)[:, : 8 * count],
+                jnp.concatenate([t1, t2, t1, t2, t3, t1], axis=0),
+                (((0,), (0,)), ((), ())),
+                preferred_element_type=jnp.float32,
+            )
+            for v in range(b + 3, count):
+                rows[v] = rows[v] - change[8 * v : 8 * (v + 1), :]
+    return [r * s for r, s in zip(rows, done)]
 
 
 def power_kernel(
-    chunks, packed_ref, start_ref, low_ref, high_ref, frames_ref, out_ref,
-    a1_ref, a2_ref, a3_ref, kept_ref, sems,
+    chunks, core_ref, own_ref, other_ref, start_ref, low_ref, high_ref, frames_ref, out_ref,
+    a1_ref, a2_ref, a3_ref, sized_ref, second_ref, kept_ref, zero_ref, sems,
 ):
     copy = functools.partial(chunk_copy, frames_ref, kept_ref, sems)
     for turn in range(chunks):
         copy(turn).start()
+    zero_ref[...] = jnp.zeros_like(zero_ref)
     down = lax.broadcasted_iota(jnp.int32, (256, 256), 0)
     across = lax.broadcasted_iota(jnp.int32, (256, 256), 1)
-    folded = jnp.concatenate([packed_ref[0:256, :], packed_ref[512:768, :]], axis=1)
-    cross = jnp.concatenate([packed_ref[256:512, :], packed_ref[768:1024, :]], axis=1)
+    first = core_ref[0] == 0
+
+    def whole(spot):
+        own, other = own_ref[spot : spot + 256, :], other_ref[spot : spot + 256, :]
+        return jnp.concatenate(
+            [jnp.where(first, own, other), jnp.where(first, other, own)], axis=1
+        )
+
+    folded, cross = whole(0), whole(256)
     turned = folded.T
     top = jnp.where(down >= across, folded, turned)
     low = jnp.where(down < across, folded, turned)
@@ -186,19 +234,39 @@
     ).astype(jnp.float32)
     none = jnp.zeros((rank, frames), jnp.bfloat16)
 
-    def sweep(turn, product):
-        parts = split(product)
-        right = [jnp.concatenate([p, none], axis=0) for p in parts]
-        grown = full_product(parts, right, 1) + unit
-        rows = eliminated([grown[8 * v : 8 * (v + 1), :] for v in range(rank // 8)])
-        factor = jnp.concatenate(rows, axis=0)
-        return full_product(split(factor), [jnp.concatenate([none, p], axis=0) for p in parts])
-
-    def iteration(turn, subspace):
-        product = full_product(split(subspace), (a1_ref[...], a2_ref[...], a3_ref[...]))
-        return lax.fori_loop(0, 2, sweep, product)
-
-    subspace = lax.fori_loop(0, ITERS, iteration, start_ref[...])
+    def under(parts):
+        return [jnp.concatenate([none[:, : p.shape[1]], p], axis=0) for p in parts]
+
+    def over(parts):
+        return [jnp.concatenate([p, none[:, : p.shape[1]]], axis=0) for p in parts]
+
+    def factor_of(gram):
+        grown = gram + unit
+        tiles = [grown[8 * v : 8 * (v + 1), :] for v in range(rank // 8)]
+        return split(jnp.concatenate(eliminated(tiles, zero_ref[...]), axis=0))
+
+    weights = (a1_ref, a2_ref, a3_ref)
+
+    def iteration(turn, carry):
+        product, gram = carry
+        sized = split(full_product(factor_of(gram), under(split(product))))
+        second = factor_of(full_product(sized, over(sized), 1))
+        for at, part in enumerate(sized):
+            sized_ref[at] = part
+        for at, part in enumerate(second):
+            second_ref[at] = part
+        ahead = split(full_product(sized, [w[...] for w in weights]))
+        square = split(full_product(ahead, under(ahead), 1))
+        product = full_product(second, under(ahead))
+        half = full_product(second, under(square))
+        return product, full_product(split(half), over(second), 1)
+
+    product = full_product(split(start_ref[...]), [w[...] for w in weights])
+    parts = split(product)
+    lax.fori_loop(0, ITERS, iteration, (product, full_product(parts, over(parts), 1)))
+    subspace = full_product(
+        [second_ref[at] for at in range(3)], under([sized_ref[at] for at in range(3)])
+    )
     rows = kept_ref.shape[0]
     subspace_low = subspace.astype(jnp.bfloat16)[:, :rows]
     component = lax.broadcasted_iota(jnp.int32, (rank, COLS), 0)
@@ -220,13 +288,15 @@
     lax.fori_loop(0, kept_ref.shape[1] // COLS, project, 0)
 
 
-def power_of(packed, start, low, high, frames):
+def power_of(core, own, other, start, low, high, frames):
     rows, columns = frames.shape[1:]
     chunks = columns // CHUNK
     return pl.pallas_call(
         functools.partial(power_kernel, chunks),
         out_shape=jax.ShapeDtypeStruct((1, columns), jnp.float32),
         in_specs=[
+            pl.BlockSpec(memory_space=pltpu.SMEM),
+            pl.BlockSpec(memory_space=pltpu.VMEM),
             pl.BlockSpec(memory_space=pltpu.VMEM),
             pl.BlockSpec(memory_space=pltpu.VMEM),
             pl.BlockSpec(memory_space=pltpu.SMEM),
@@ -235,14 +305,20 @@
         ],
         out_specs=pl.BlockSpec(memory_space=pltpu.VMEM),
         scratch_shapes=[pltpu.VMEM((512, 512), jnp.bfloat16)] * 3
-        + [pltpu.VMEM((rows, columns), frames.dtype), pltpu.SemaphoreType.DMA((chunks,))],
-        compiler_params=pltpu.CompilerParams(vmem_limit_bytes=56 * 2**20),
+        + [
+            pltpu.VMEM((3, 64, 512), jnp.bfloat16),
+            pltpu.VMEM((3, 64, 128), jnp.bfloat16),
+            pltpu.VMEM((rows, columns), frames.dtype),
+            pltpu.VMEM((8, 128), jnp.float32),
+            pltpu.SemaphoreType.DMA((chunks,)),
+        ],
+        compiler_params=pltpu.CompilerParams(vmem_limit_bytes=40 * 2**20),
         name="power",
-    )(packed, start, low, high, frames)
+    )(core, own, other, start, low, high, frames)
 
 
 def tile_rates(decay):
-    steps, group = lax.axis_size("tm"), lax.axis_size("vox")
+    steps, group = lax.axis_size("tm"), lax.axis_size("chip")
     step = lax.axis_index("tm")
     turns = [decay] + [
         lax.ppermute(decay, "tm", [(i, (i + k) % steps) for i in range(steps)])
@@ -256,9 +332,8 @@
         every.append(mine)
     rates = jnp.stack(every)
     rates = jnp.pad(rates, ((0, 0), (0, 512 - rates.shape[1])))
-    tile = step * group + lax.axis_index("vox")
-    first_row = 8 * (tile % 64)
-    first_column = 128 * (tile // 64)
+    first_row = 8 * (step * group + lax.axis_index("chip"))
+    first_column = 128 * lax.axis_index("core")
     row = first_row + lax.broadcasted_iota(jnp.int32, (8, 128), 0)
     column = first_column + lax.broadcasted_iota(jnp.int32, (8, 128), 1)
 
@@ -278,17 +353,32 @@
     )
 
 
+def swapped(x):
+    return lax.ppermute(x, "core", [(0, 1), (1, 0)])
+
+
+def exchanged(tiles):
+    return lax.all_to_all(tiles, ("tm", "chip"), 0, 0, tiled=True)
+
+
 def per_device(frames, decay, start, clutter_cut, noise_cut):
+    core = lax.axis_index("core").reshape(1)
     rates = tile_rates(decay[0])
-    packed = local_gram(frames)
-    parts = lax.all_to_all(packed.reshape(128, 8, 128), ("tm", "vox"), 0, 0, tiled=True)
-    held = lax.all_to_all(chain(parts, rates), ("tm", "vox"), 0, 0, tiled=True)
+    own, other = local_gram(core, frames)
+    tiles = (own + swapped(other)).reshape(64, 8, 128)
+    parts = exchanged(tiles)
+    held = chain(parts, rates)
+    own = exchanged(held)
     begin = jnp.pad(start.T, ((0, 0), (0, 512 - start.shape[0])))
-    return power_of(held.reshape(1024, 128), begin, clutter_cut, noise_cut, frames)
+    other = swapped(own)
+    own, other = own.reshape(512, 128), other.reshape(512, 128)
+    return power_of(core, own, other, begin, clutter_cut, noise_cut, frames)
 
 
 def solution(mesh):
-    placed = (P("tm", None, "vox"), P("tm", None), P(), P("tm"), P("tm"))
+    chips = Mesh(mesh.devices.reshape(4, 16, 2), ("tm", "chip", "core"))
+    over = ("chip", "core")
+    placed = (P("tm", None, over), P("tm", None), P(), P("tm"), P("tm"))
     return jax.shard_map(
-        per_device, mesh=mesh, in_specs=placed, out_specs=P("tm", "vox"), check_vma=False
+        per_device, mesh=chips, in_specs=placed, out_specs=P("tm", over), check_vma=False
     )

time: 95.6 us -> 80.4 us (0.84)
  waiting for transfers between devices: 24.8 us -> 10.8 us
  Pallas kernels: 47.5 us -> 33.7 us
  blocking collectives: 0 us -> 13.7 us
  local copies, waits for them, and re-layouts: 1.56 us -> 0.1 us
    all_to_all x2 -> x1, waiting for transfers between devices: 24.8 us -> 9.83 us  [exchanged(): return lax.all_to_all(tiles, ('tm', 'chip'), 0, 0, tiled=True)]
    all_to_all x0 -> x1, blocking collectives: none -> 13.7 us  [exchanged(): return lax.all_to_all(tiles, ('tm', 'chip'), 0, 0, tiled=True)]
    pallas_call x1, Pallas kernels: 36 us -> 23.8 us  [power_of(): pl.pallas_call(functools.partial(power_kernel, chunks), out_shape=jax.Sha...]
    all_to_all x2 -> x1, starting transfers between devices: 15.2 us -> 10.2 us  [exchanged(): return lax.all_to_all(tiles, ('tm', 'chip'), 0, 0, tiled=True)]
    ppermute x0 -> x2, starting transfers between devices: none -> 4.71 us  [swapped(): return lax.ppermute(x, 'core', [(0, 1), (1, 0)])]
  transfers between devices with their start and end apart: 5 -> 6, of which waited for: 2 -> 2; matrix products, arithmetic and copies ran while one was open for 1% -> 0% of each run, Pallas kernels for 11% -> 12%
where the time goes in v2:
time: 80.4 us; the launch traced here: 80.2 us
  Pallas kernels  33.7 us (42%)
  starting transfers between devices  19.5 us (24%)
  blocking collectives  13.7 us (17%)
  waiting for transfers between devices  10.8 us (13%)
  between operations  1.43 us (2%)
  other arithmetic  0.96 us (1%)
    pallas_call x1, Pallas kernels, power_of(): pl.pallas_call(functools.partial(power_kernel, chunks), out_shape=jax.Sha...  23.8 us
    all_to_all x1, blocking collectives, exchanged(): return lax.all_to_all(tiles, ('tm', 'chip'), 0, 0, tiled=True)  13.7 us
    all_to_all x1, starting transfers between devices, exchanged(): return lax.all_to_all(tiles, ('tm', 'chip'), 0, 0, tiled=True)  10.2 us
    pallas_call x1, Pallas kernels, local_gram(): pl.pallas_call(functools.partial(gram_kernel, chunks), out_shape=[pltpu.V...  9.86 us
    all_to_all x1, waiting for transfers between devices, exchanged(): return lax.all_to_all(tiles, ('tm', 'chip'), 0, 0, tiled=True)  9.83 us
    ppermute x2, starting transfers between devices, swapped(): return lax.ppermute(x, 'core', [(0, 1), (1, 0)])  4.71 us
    ppermute x3, starting transfers between devices, tile_rates(): lax.ppermute(decay, 'tm', [(i, (i + k) % steps) for i in range(steps)])  4.59 us
  transfers between devices with their start and end apart: 6, of which 2 were waited for; matrix products, arithmetic and copies ran while one was open for 0% of the time, Pallas kernels for 12%

profile of v2, /device:TPU:1, one launch (start us, length us, event | category | flops | bytes accessed | tf_op | source)
XLA Modules:
  0.0 80.2 jit_solution(5977011096680950241)
XLA Ops:
  0.0 0.0 copy-start.1
  0.0 0.0 copy-start
  0.0 3.6 %collective-permute-start.3 = (f32[500]{0:T(512)}, f32[500]{0:T(512)S(1)}, u32[]{:S(2)}, u32[]{:S(2)}) collective-permute-start(f32[500]{0:T(512)} %bitcast.14), channel_id=1, source_target_pairs={{0,96},{32,0},{64,32},{96,64},{1,97},{33,1},{65,33},{97,65},{2,98}... | collective-permute-start | bytes 6008 | tf_op jit(solution)/shard_map/ppermute | solution.py:324
  3.6 0.3 collective-permute-start.2
  3.9 0.7 collective-permute-start.1
  4.6 9.9 %local_gram.1 = (f32[512,128]{1,0:T(8,128)S(1)}, f32[512,128]{1,0:T(8,128)S(1)}) custom-call(s32[1]{0:T(128)} %bitcast.core_ref, bf16[1,500,16384]{2,1,0:T(8,128)(2,1)} %frames_ref.3), custom_call_target="tpu_custom_call" | custom-call | flops 8192000000 | bytes 16384000 | tf_op jit(solution)/shard_map/local_gram/pallas_call | solution.py:62
  14.5 1.6 %collective-permute-start = (f32[512,128]{1,0:T(8,128)S(1)}, f32[512,128]{1,0:T(8,128)S(1)}, u32[]{:S(2)}, u32[]{:S(2)}) collective-permute-start(f32[512,128]{1,0:T(8,128)S(1)} %get-tuple-element.8), channel_id=1, source_target_pairs={{0,1},{1,0},{2,3},{3,2},{4,5},{5,4},{6,7},{7,6},{8,9},{9,8},{10,11... | collective-permute-start | bytes 786440 | tf_op jit(solution)/shard_map/ppermute | solution.py:357
  16.1 0.1 compare_or_fusion
  16.2 0.0 collective-permute-done.3
  16.2 0.0 collective-permute-done.2
  16.2 0.0 collective-permute-done.1
  16.2 0.0 copy-done.1
  16.3 0.9 %collective-permute-done = f32[512,128]{1,0:T(8,128)S(1)} collective-permute-done((f32[512,128]{1,0:T(8,128)S(1)}, f32[512,128]{1,0:T(8,128)S(1)}, u32[]{:S(2)}, u32[]{:S(2)}) %collective-permute-start) | collective-permute-done | bytes 262176 | tf_op jit(solution)/shard_map/ppermute | solution.py:357
  17.2 0.7 add_bitcast_fusion
  18.0 10.2 %all-to-all-start = ((f32[64,8,128]{2,1,0:T(8,128)}), f32[64,8,128]{2,1,0:T(8,128)S(1)}, u32[]{:S(2)}, u32[]{:S(2)}) async-start(f32[64,8,128]{2,1,0:T(8,128)} %add_bitcast_fusion), calls=%async_computation | async-start | bytes 524288 | tf_op jit(solution)/shard_map/all_to_all | solution.py:361
  28.2 0.1 constant_dynamic-slice_fusion.2
  28.3 0.1 select_select_fusion.rates_ref
  28.3 9.8 %all-to-all-done.parts_ref = f32[64,8,128]{2,1,0:T(8,128)S(1)} async-done(((f32[64,8,128]{2,1,0:T(8,128)}), f32[64,8,128]{2,1,0:T(8,128)S(1)}, u32[]{:S(2)}, u32[]{:S(2)}) %all-to-all-start) | async-done | bytes 262176 | tf_op jit(solution)/shard_map/all_to_all | solution.py:361
  38.2 13.7 %all_to_all.10 = f32[64,8,128]{2,1,0:T(8,128)S(1)} all-to-all(f32[64,8,128]{2,1,0:T(8,128)S(1)} %chain.1), channel_id=1, replica_groups=mesh['tm'=4,'chip'=16,'core'=2] {'tm','chip'}, dimensions={0} | all-to-all | bytes 524288 | tf_op jit(solution)/shard_map/all_to_all | solution.py:361
  51.9 3.1 %collective-permute-start.4 = (f32[64,8,128]{2,1,0:T(8,128)S(1)}, f32[64,8,128]{2,1,0:T(8,128)S(1)}, u32[]{:S(2)}, u32[]{:S(2)}) collective-permute-start(f32[64,8,128]{2,1,0:T(8,128)S(1)} %all_to_all.10), channel_id=1, source_target_pairs={{0,1},{1,0},{2,3},{3,2},{4,5},{5,4},{6,7},{7,6},{8,9},{9,8},{10,11... | collective-permute-start | bytes 786440 | tf_op jit(solution)/shard_map/ppermute | solution.py:357
  56.3 0.0 copy-done
  56.4 0.0 collective-permute-done.4
  56.4 23.8 %power.1 = f32[1,16384]{1,0:T(1,128)} custom-call(s32[1]{0:T(128)} %bitcast.core_ref, f32[512,128]{1,0:T(8,128)S(1)} %bitcast.11, f32[512,128]{1,0:T(8,128)S(1)} %bitcast.12, f32[64,512]{1,0:T(8,128)S(1)} %pad.9.start_ref, s32[1]{0:T(128)S(6)} %copy.6.low_ref, s32[1]{0:T(128)S(6)} %copy.7.high_ref, bf16[1,500,16384]{2,1,0:T(8,128)(2,1)} %frames_ref.3), custom_call_target="tpu_custom_call" | custom-call | tf_op jit(solution)/shard_map/power/pallas_call | solution.py:294
  (10 shorter events, 0.1 us)
Async XLA Ops:
  0.0 16.2 %copy-start.1 = (f32[1,500]{1,0:T(1,128)S(1)}, f32[1,500]{1,0:T(1,128)}, u32[]{:S(2)}) copy-start(f32[1,500]{1,0:T(1,128)} %param.6) | copy-start | bytes 6004
  0.0 56.3 %copy-start = (f32[500,64]{0,1:T(8,128)S(1)}, f32[500,64]{0,1:T(8,128)}, u32[]{:S(2)}) copy-start(f32[500,64]{0,1:T(8,128)} %param.7) | copy-start | bytes 384004
  0.0 16.2 %collective-permute-start.3 = (f32[500]{0:T(512)}, f32[500]{0:T(512)S(1)}, u32[]{:S(2)}, u32[]{:S(2)}) collective-permute-start(f32[500]{0:T(512)} %bitcast.14), channel_id=1, source_target_pairs={{0,96},{32,0},{64,32},{96,64},{1,97},{33,1},{65,33},{97,65},{2,98}... | collective-permute-start | bytes 6008 | tf_op jit(solution)/shard_map/ppermute | solution.py:324
  3.6 12.6 %collective-permute-start.2 = (f32[500]{0:T(512)}, f32[500]{0:T(512)S(1)}, u32[]{:S(2)}, u32[]{:S(2)}) collective-permute-start(f32[500]{0:T(512)} %bitcast.15), channel_id=1, source_target_pairs={{0,64},{32,96},{64,0},{96,32},{1,65},{33,97},{65,1},{97,33},{2,66}... | collective-permute-start | bytes 6008 | tf_op jit(solution)/shard_map/ppermute | solution.py:324
  3.9 12.3 %collective-permute-start.1 = (f32[500]{0:T(512)}, f32[500]{0:T(512)S(1)}, u32[]{:S(2)}, u32[]{:S(2)}) collective-permute-start(f32[500]{0:T(512)} %bitcast.16), channel_id=1, source_target_pairs={{0,32},{32,64},{64,96},{96,0},{1,33},{33,65},{65,97},{97,1},{2,34}... | collective-permute-start | bytes 6008 | tf_op jit(solution)/shard_map/ppermute | solution.py:324
  14.5 2.8 %collective-permute-start = (f32[512,128]{1,0:T(8,128)S(1)}, f32[512,128]{1,0:T(8,128)S(1)}, u32[]{:S(2)}, u32[]{:S(2)}) collective-permute-start(f32[512,128]{1,0:T(8,128)S(1)} %get-tuple-element.8), channel_id=1, source_target_pairs={{0,1},{1,0},{2,3},{3,2},{4,5},{5,4},{6,7},{7,6},{8,9},{9,8},{10,11... | collective-permute-start | bytes 786440 | tf_op jit(solution)/shard_map/ppermute | solution.py:357
  18.0 20.2 %all-to-all-start = ((f32[64,8,128]{2,1,0:T(8,128)}), f32[64,8,128]{2,1,0:T(8,128)S(1)}, u32[]{:S(2)}, u32[]{:S(2)}) async-start(f32[64,8,128]{2,1,0:T(8,128)} %add_bitcast_fusion), calls=%async_computation | async-start | bytes 524288 | tf_op jit(solution)/shard_map/all_to_all | solution.py:361
  51.9 4.5 %collective-permute-start.4 = (f32[64,8,128]{2,1,0:T(8,128)S(1)}, f32[64,8,128]{2,1,0:T(8,128)S(1)}, u32[]{:S(2)}, u32[]{:S(2)}) collective-permute-start(f32[64,8,128]{2,1,0:T(8,128)S(1)} %all_to_all.10), channel_id=1, source_target_pairs={{0,1},{1,0},{2,3},{3,2},{4,5},{5,4},{6,7},{7,6},{8,9},{9,8},{10,11... | collective-permute-start | bytes 786440 | tf_op jit(solution)/shard_map/ppermute | solution.py:357

commit v3 on v2

--- a/solution.py
+++ b/solution.py
@@ -10,21 +10,21 @@
 
 ITERS = 6
 CHUNK = 2048
+DEPTH = 3
 COLS = 4096
 
 
 def chunk_copy(frames_ref, kept_ref, sems, turn):
-    span = pl.ds(turn * CHUNK, CHUNK)
+    span = pl.ds(pl.multiple_of(turn * CHUNK, CHUNK), CHUNK)
     return pltpu.make_async_copy(frames_ref.at[0, :, span], kept_ref.at[:, span], sems.at[turn])
 
 
-def gram_kernel(chunks, core_ref, frames_ref, own_ref, other_ref, kept_ref, top_ref, cross_ref, low_ref, sems):
+def gram_kernel(chunks, frames_ref, packed_ref, kept_ref, left_ref, low_ref, sems):
     copy = functools.partial(chunk_copy, frames_ref, kept_ref, sems)
 
-    for turn in range(chunks):
+    for turn in range(DEPTH):
         copy(turn).start()
-    top_ref[...] = jnp.zeros_like(top_ref)
-    cross_ref[...] = jnp.zeros_like(cross_ref)
+    left_ref[...] = jnp.zeros_like(left_ref)
     low_ref[...] = jnp.zeros_like(low_ref)
     rows = kept_ref.shape[0]
     rest = rows - 256
@@ -34,11 +34,15 @@
 
     def one(turn, carry):
         copy(turn).wait()
+
+        @pl.when(turn + DEPTH < chunks)
+        def _():
+            copy(turn + DEPTH).start()
+
         span = pl.ds(pl.multiple_of(turn * CHUNK, CHUNK), CHUNK)
         upper = kept_ref[0:256, span]
         lower = kept_ref[256:rows, span]
-        top_ref[...] += product(upper, upper)
-        cross_ref[0:rest, :] += product(lower, upper)
+        left_ref[0:rows, :] += product(kept_ref[:, span], upper)
         low_ref[0:rest, 0:rest] += product(lower, lower)
         return carry
 
@@ -46,28 +50,27 @@
     down = lax.broadcasted_iota(jnp.int32, (256, 256), 0)
     across = lax.broadcasted_iota(jnp.int32, (256, 256), 1)
     low = low_ref[...]
-    folded = jnp.where(down >= across, top_ref[...], low)
+    folded = jnp.where(down >= across, left_ref[0:256, :], low)
     diagonal = jnp.sum(jnp.where(down == across, low, 0.0), axis=0, keepdims=True)
-    cross = jnp.where(down == 255, jnp.broadcast_to(diagonal, (256, 256)), cross_ref[...])
-    first = core_ref[0] == 0
-    for spot, piece in ((0, folded), (256, cross)):
-        left, right = piece[:, :128], piece[:, 128:]
-        own_ref[spot : spot + 256, :] = jnp.where(first, left, right)
-        other_ref[spot : spot + 256, :] = jnp.where(first, right, left)
-
-
-def local_gram(core, frames):
+    cross = jnp.where(down == 255, jnp.broadcast_to(diagonal, (256, 256)), left_ref[256:512, :])
+    for spot, piece in ((0, folded), (32, cross)):
+        for half in range(2):
+            packed_ref[spot : spot + 32, half] = piece[:, 128 * half : 128 * (half + 1)].reshape(
+                32, 8, 128
+            )
+
+
+def local_gram(frames):
     rows, columns = frames.shape[1:]
     chunks = columns // CHUNK
     return pl.pallas_call(
         functools.partial(gram_kernel, chunks),
-        out_shape=[pltpu.VMEM((512, 128), jnp.float32)] * 2,
-        in_specs=[pl.BlockSpec(memory_space=pltpu.SMEM), pl.BlockSpec(memory_space=pltpu.HBM)],
-        out_specs=[pl.BlockSpec(memory_space=pltpu.VMEM)] * 2,
+        out_shape=jax.ShapeDtypeStruct((64, 2, 8, 128), jnp.float32),
+        in_specs=[pl.BlockSpec(memory_space=pltpu.HBM)],
+        out_specs=pl.BlockSpec(memory_space=pltpu.VMEM),
         scratch_shapes=[
             pltpu.VMEM((rows, columns), frames.dtype),
-            pltpu.VMEM((256, 256), jnp.float32),
-            pltpu.VMEM((256, 256), jnp.float32),
+            pltpu.VMEM((512, 256), jnp.float32),
             pltpu.VMEM((256, 256), jnp.float32),
             pltpu.SemaphoreType.DMA((chunks,)),
         ],
@@ -76,22 +79,24 @@
             flops=2 * rows * rows * columns, bytes_accessed=2 * rows * columns, transcendentals=0
         ),
         name="local_gram",
-    )(core, frames)
-
-
-def chain_kernel(steps, group, parts_ref, rates_ref, out_ref):
+    )(frames)
+
+
+def chain_kernel(steps, group, copies, parts_ref, rates_ref, out_ref):
     held = None
     for step in range(steps):
         part = jnp.sum(parts_ref[step * group : (step + 1) * group], axis=0)
         held = part if step == 0 else rates_ref[step] * held + part
-        out_ref[step * group : (step + 1) * group] = jnp.broadcast_to(held[None], (group, 8, 128))
-
-
-def chain(parts, rates):
+        out_ref[step * copies : (step + 1) * copies] = jnp.broadcast_to(
+            held[None], (copies, 8, 128)
+        )
+
+
+def chain(parts, rates, copies):
     steps = rates.shape[0]
     return pl.pallas_call(
-        functools.partial(chain_kernel, steps, parts.shape[0] // steps),
-        out_shape=jax.ShapeDtypeStruct(parts.shape, parts.dtype),
+        functools.partial(chain_kernel, steps, parts.shape[0] // steps, copies),
+        out_shape=jax.ShapeDtypeStruct((steps * copies, 8, 128), parts.dtype),
         compiler_params=pltpu.CompilerParams(vmem_limit_bytes=4 * 2**20),
         name="chain",
     )(parts, rates)
@@ -268,9 +273,9 @@
         [second_ref[at] for at in range(3)], under([sized_ref[at] for at in range(3)])
     )
     rows = kept_ref.shape[0]
-    subspace_low = subspace.astype(jnp.bfloat16)[:, :rows]
-    component = lax.broadcasted_iota(jnp.int32, (rank, COLS), 0)
+    component = lax.broadcasted_iota(jnp.int32, subspace.shape, 0)
     band = (component >= low_ref[0]) & (component < high_ref[0])
+    subspace_low = jnp.where(band, subspace, 0.0).astype(jnp.bfloat16)[:, :rows]
 
     def arrive(turn, carry):
         copy(turn).wait()
@@ -281,7 +286,6 @@
     def project(turn, carry):
         span = pl.ds(pl.multiple_of(turn * COLS, COLS), COLS)
         values = mul(subspace_low, kept_ref[:, span])
-        values = jnp.where(band, values, 0.0)
         out_ref[:, span] = jnp.sum(values * values, axis=0, keepdims=True) / rows
         return carry
 
@@ -357,18 +361,17 @@
     return lax.ppermute(x, "core", [(0, 1), (1, 0)])
 
 
-def exchanged(tiles):
-    return lax.all_to_all(tiles, ("tm", "chip"), 0, 0, tiled=True)
+def exchanged(tiles, axes):
+    return lax.all_to_all(tiles, axes, 0, 0, tiled=True)
 
 
 def per_device(frames, decay, start, clutter_cut, noise_cut):
     core = lax.axis_index("core").reshape(1)
     rates = tile_rates(decay[0])
-    own, other = local_gram(core, frames)
-    tiles = (own + swapped(other)).reshape(64, 8, 128)
-    parts = exchanged(tiles)
-    held = chain(parts, rates)
-    own = exchanged(held)
+    packed = local_gram(frames)
+    parts = exchanged(packed.reshape(128, 8, 128), ("tm", "chip", "core"))
+    held = chain(parts, rates, lax.axis_size("chip"))
+    own = exchanged(held, ("tm", "chip"))
     begin = jnp.pad(start.T, ((0, 0), (0, 512 - start.shape[0])))
     other = swapped(own)
     own, other = own.reshape(512, 128), other.reshape(512, 128)

time: 80.4 us -> 81.3 us (1.011)
  waiting for transfers between devices: 10.8 us -> 13.2 us
  starting transfers between devices: 19.5 us -> 17.8 us
    all_to_all x1, waiting for transfers between devices: 9.83 us -> 13.2 us  [exchanged(): return lax.all_to_all(tiles, axes, 0, 0, tiled=True)]
    ppermute x2 -> x1, starting transfers between devices: 4.71 us -> 2.62 us  [swapped(): return lax.ppermute(x, 'core', [(0, 1), (1, 0)])]
    ppermute x2 -> x1, waiting for transfers between devices: 0.93 us -> 0.01 us  [swapped(): return lax.ppermute(x, 'core', [(0, 1), (1, 0)])]
  transfers between devices with their start and end apart: 6 -> 5, of which waited for: 2 -> 1; matrix products, arithmetic and copies ran while one was open for 0% -> 0% of each run, Pallas kernels for 12% -> 13%
where the time goes in v3:
time: 81.3 us; the launch traced here: 81.1 us
  Pallas kernels  34.5 us (42%)
  starting transfers between devices  17.8 us (22%)
  blocking collectives  13.8 us (17%)
  waiting for transfers between devices  13.2 us (16%)
  between operations  1.49 us (2%)
    pallas_call x1, Pallas kernels, power_of(): pl.pallas_call(functools.partial(power_kernel, chunks), out_shape=jax.Sha...  23.8 us
    all_to_all x1, blocking collectives, exchanged(): return lax.all_to_all(tiles, axes, 0, 0, tiled=True)  13.8 us
    all_to_all x1, waiting for transfers between devices, exchanged(): return lax.all_to_all(tiles, axes, 0, 0, tiled=True)  13.2 us
    pallas_call x1, Pallas kernels, local_gram(): pl.pallas_call(functools.partial(gram_kernel, chunks), out_shape=jax.Shap...  10.6 us
    all_to_all x1, starting transfers between devices, exchanged(): return lax.all_to_all(tiles, axes, 0, 0, tiled=True)  10.6 us
    ppermute x3, starting transfers between devices, tile_rates(): lax.ppermute(decay, 'tm', [(i, (i + k) % steps) for i in range(steps)])  4.59 us
    ppermute x1, starting transfers between devices, swapped(): return lax.ppermute(x, 'core', [(0, 1), (1, 0)])  2.62 us
  transfers between devices with their start and end apart: 5, of which 1 were waited for; matrix products, arithmetic and copies ran while one was open for 0% of the time, Pallas kernels for 13%

profile of v3, /device:TPU:1, one launch (start us, length us, event | category | flops | bytes accessed | tf_op | source)
XLA Modules:
  0.0 81.1 jit_solution(4514197053412190279)
XLA Ops:
  0.0 0.0 copy-start.1
  0.0 0.0 copy-start
  0.0 3.6 %collective-permute-start.2 = (f32[500]{0:T(512)}, f32[500]{0:T(512)S(1)}, u32[]{:S(2)}, u32[]{:S(2)}) collective-permute-start(f32[500]{0:T(512)} %bitcast.14), channel_id=1, source_target_pairs={{0,96},{32,0},{64,32},{96,64},{1,97},{33,1},{65,33},{97,65},{2,98}... | collective-permute-start | bytes 6008 | tf_op jit(solution)/shard_map/ppermute | solution.py:328
  3.6 0.3 collective-permute-start.1
  3.9 0.7 collective-permute-start
  4.6 10.6 %local_gram.1 = f32[64,2,8,128]{3,2,1,0:T(8,128)} custom-call(bf16[1,500,16384]{2,1,0:T(8,128)(2,1)} %frames_ref.3), custom_call_target="tpu_custom_call" | custom-call | flops 8192000000 | bytes 16384000 | tf_op jit(solution)/shard_map/local_gram/pallas_call | solution.py:66
  15.2 10.6 %all-to-all-start = ((f32[128,8,128]{2,1,0:T(8,128)}), f32[128,8,128]{2,1,0:T(8,128)S(1)}, u32[]{:S(2)}, u32[]{:S(2)}) async-start(f32[128,8,128]{2,1,0:T(8,128)} %bitcast.12), calls=%async_computation | async-start | bytes 1048576 | tf_op jit(solution)/shard_map/all_to_all | solution.py:365
  26.0 0.1 compare_or_fusion
  26.0 0.0 collective-permute-done.2
  26.0 0.0 collective-permute-done.1
  26.0 0.0 collective-permute-done
  26.1 0.0 copy-done.1
  26.1 0.1 constant_dynamic-slice_fusion.2
  26.2 0.1 select_select_fusion.rates_ref
  26.3 13.2 %all-to-all-done.parts_ref = f32[128,8,128]{2,1,0:T(8,128)S(1)} async-done(((f32[128,8,128]{2,1,0:T(8,128)}), f32[128,8,128]{2,1,0:T(8,128)S(1)}, u32[]{:S(2)}, u32[]{:S(2)}) %all-to-all-start) | async-done | bytes 524320 | tf_op jit(solution)/shard_map/all_to_all | solution.py:365
  39.4 0.1 chain.1
  39.5 13.8 %all_to_all.10 = f32[64,8,128]{2,1,0:T(8,128)S(1)} all-to-all(f32[64,8,128]{2,1,0:T(8,128)S(1)} %chain.1), channel_id=1, replica_groups=mesh['tm'=4,'chip'=16,'core'=2] {'tm','chip'}, dimensions={0} | all-to-all | bytes 524288 | tf_op jit(solution)/shard_map/all_to_all | solution.py:365
  53.3 2.6 %collective-permute-start.3 = (f32[64,8,128]{2,1,0:T(8,128)S(1)}, f32[64,8,128]{2,1,0:T(8,128)S(1)}, u32[]{:S(2)}, u32[]{:S(2)}) collective-permute-start(f32[64,8,128]{2,1,0:T(8,128)S(1)} %all_to_all.10), channel_id=1, source_target_pairs={{0,1},{1,0},{2,3},{3,2},{4,5},{5,4},{6,7},{7,6},{8,9},{9,8},{10,11... | collective-permute-start | bytes 786440 | tf_op jit(solution)/shard_map/ppermute | solution.py:361
  57.2 0.0 copy-done
  57.3 0.0 collective-permute-done.3
  57.3 23.8 %power.1 = f32[1,16384]{1,0:T(1,128)} custom-call(s32[1]{0:T(128)} %bitcast.core_ref, f32[512,128]{1,0:T(8,128)S(1)} %bitcast.10, f32[512,128]{1,0:T(8,128)S(1)} %bitcast.11, f32[64,512]{1,0:T(8,128)S(1)} %pad.9.start_ref, s32[1]{0:T(128)S(6)} %copy.6.low_ref, s32[1]{0:T(128)S(6)} %copy.7.high_ref, bf16[1,500,16384]{2,1,0:T(8,128)(2,1)} %frames_ref.3), custom_call_target="tpu_custom_call" | custom-call | tf_op jit(solution)/shard_map/power/pallas_call | solution.py:298
  (9 shorter events, 0.1 us)
Async XLA Ops:
  0.0 26.1 %copy-start.1 = (f32[1,500]{1,0:T(1,128)S(1)}, f32[1,500]{1,0:T(1,128)}, u32[]{:S(2)}) copy-start(f32[1,500]{1,0:T(1,128)} %param.6) | copy-start | bytes 6004
  0.0 57.2 %copy-start = (f32[500,64]{0,1:T(8,128)S(1)}, f32[500,64]{0,1:T(8,128)}, u32[]{:S(2)}) copy-start(f32[500,64]{0,1:T(8,128)} %param.7) | copy-start | bytes 384004
  0.0 26.0 %collective-permute-start.2 = (f32[500]{0:T(512)}, f32[500]{0:T(512)S(1)}, u32[]{:S(2)}, u32[]{:S(2)}) collective-permute-start(f32[500]{0:T(512)} %bitcast.14), channel_id=1, source_target_pairs={{0,96},{32,0},{64,32},{96,64},{1,97},{33,1},{65,33},{97,65},{2,98}... | collective-permute-start | bytes 6008 | tf_op jit(solution)/shard_map/ppermute | solution.py:328
  3.6 22.5 %collective-permute-start.1 = (f32[500]{0:T(512)}, f32[500]{0:T(512)S(1)}, u32[]{:S(2)}, u32[]{:S(2)}) collective-permute-start(f32[500]{0:T(512)} %bitcast.15), channel_id=1, source_target_pairs={{0,64},{32,96},{64,0},{96,32},{1,65},{33,97},{65,1},{97,33},{2,66}... | collective-permute-start | bytes 6008 | tf_op jit(solution)/shard_map/ppermute | solution.py:328
  3.9 22.1 %collective-permute-start = (f32[500]{0:T(512)}, f32[500]{0:T(512)S(1)}, u32[]{:S(2)}, u32[]{:S(2)}) collective-permute-start(f32[500]{0:T(512)} %bitcast.16), channel_id=1, source_target_pairs={{0,32},{32,64},{64,96},{96,0},{1,33},{33,65},{65,97},{97,1},{2,34}... | collective-permute-start | bytes 6008 | tf_op jit(solution)/shard_map/ppermute | solution.py:328
  15.2 24.2 %all-to-all-start = ((f32[128,8,128]{2,1,0:T(8,128)}), f32[128,8,128]{2,1,0:T(8,128)S(1)}, u32[]{:S(2)}, u32[]{:S(2)}) async-start(f32[128,8,128]{2,1,0:T(8,128)} %bitcast.12), calls=%async_computation | async-start | bytes 1048576 | tf_op jit(solution)/shard_map/all_to_all | solution.py:365
  53.3 4.0 %collective-permute-start.3 = (f32[64,8,128]{2,1,0:T(8,128)S(1)}, f32[64,8,128]{2,1,0:T(8,128)S(1)}, u32[]{:S(2)}, u32[]{:S(2)}) collective-permute-start(f32[64,8,128]{2,1,0:T(8,128)S(1)} %all_to_all.10), channel_id=1, source_target_pairs={{0,1},{1,0},{2,3},{3,2},{4,5},{5,4},{6,7},{7,6},{8,9},{9,8},{10,11... | collective-permute-start | bytes 786440 | tf_op jit(solution)/shard_map/ppermute | solution.py:361

commit v4 on v3

--- a/solution.py
+++ b/solution.py
@@ -10,7 +10,6 @@
 
 ITERS = 6
 CHUNK = 2048
-DEPTH = 3
 COLS = 4096
 
 
@@ -22,7 +21,7 @@
 def gram_kernel(chunks, frames_ref, packed_ref, kept_ref, left_ref, low_ref, sems):
     copy = functools.partial(chunk_copy, frames_ref, kept_ref, sems)
 
-    for turn in range(DEPTH):
+    for turn in range(chunks):
         copy(turn).start()
     left_ref[...] = jnp.zeros_like(left_ref)
     low_ref[...] = jnp.zeros_like(low_ref)
@@ -34,11 +33,6 @@
 
     def one(turn, carry):
         copy(turn).wait()
-
-        @pl.when(turn + DEPTH < chunks)
-        def _():
-            copy(turn + DEPTH).start()
-
         span = pl.ds(pl.multiple_of(turn * CHUNK, CHUNK), CHUNK)
         upper = kept_ref[0:256, span]
         lower = kept_ref[256:rows, span]
@@ -65,7 +59,7 @@
     chunks = columns // CHUNK
     return pl.pallas_call(
         functools.partial(gram_kernel, chunks),
-        out_shape=jax.ShapeDtypeStruct((64, 2, 8, 128), jnp.float32),
+        out_shape=pltpu.VMEM((64, 2, 8, 128), jnp.float32),
         in_specs=[pl.BlockSpec(memory_space=pltpu.HBM)],
         out_specs=pl.BlockSpec(memory_space=pltpu.VMEM),
         scratch_shapes=[
@@ -129,14 +123,14 @@
     return jnp.broadcast_to(x[index : index + 1, :], x.shape)
 
 
-def eliminated(rows, none):
+def eliminated(rows, none, start):
     rows = list(rows)
     count = len(rows)
     sub = lax.broadcasted_iota(jnp.int32, (8, 128), 0)
 
     def columns_of(v, first, size):
         return [
-            jnp.broadcast_to(rows[v][:, first + k : first + k + 1], (8, 128))
+            jnp.broadcast_to(rows[v][:, start + first + k : start + first + k + 1], (8, 128))
             for k in range(size)
         ]
 
@@ -188,19 +182,19 @@
                 jnp.concatenate([rows[a] * scales[0], rows[b] * scales[1]], axis=0)
             )
             change = lax.dot_general(
-                jnp.concatenate([u1, u1, u2, u2, u1, u3], axis=0)[:, : 8 * count],
+                jnp.concatenate([u1, u1, u2, u2, u1, u3], axis=0)[:, : start + 8 * count],
                 jnp.concatenate([t1, t2, t1, t2, t3, t1], axis=0),
                 (((0,), (0,)), ((), ())),
                 preferred_element_type=jnp.float32,
             )
             for v in range(b + 3, count):
-                rows[v] = rows[v] - change[8 * v : 8 * (v + 1), :]
+                rows[v] = rows[v] - change[start + 8 * v : start + 8 * (v + 1), :]
     return [r * s for r, s in zip(rows, done)]
 
 
 def power_kernel(
     chunks, core_ref, own_ref, other_ref, start_ref, low_ref, high_ref, frames_ref, out_ref,
-    a1_ref, a2_ref, a3_ref, sized_ref, second_ref, kept_ref, zero_ref, sems,
+    a1_ref, a2_ref, a3_ref, kept_ref, zero_ref, sems,
 ):
     copy = functools.partial(chunk_copy, frames_ref, kept_ref, sems)
     for turn in range(chunks):
@@ -233,10 +227,8 @@
     put(cross.T, 0, 1)
 
     rank, frames = start_ref.shape
-    beside = lax.broadcasted_iota(jnp.int32, (rank, 128), 0) + rank
-    unit = jnp.where(
-        lax.broadcasted_iota(jnp.int32, (rank, 128), 1) == beside, 1.0, 0.0
-    ).astype(jnp.float32)
+    line = lax.broadcasted_iota(jnp.int32, (rank, 128), 0)
+    lane = lax.broadcasted_iota(jnp.int32, (rank, 128), 1)
     none = jnp.zeros((rank, frames), jnp.bfloat16)
 
     def under(parts):
@@ -245,33 +237,29 @@
     def over(parts):
         return [jnp.concatenate([p, none[:, : p.shape[1]]], axis=0) for p in parts]
 
-    def factor_of(gram):
-        grown = gram + unit
+    def factor_of(gram, start=0):
+        grown = jnp.where(lane == line + (rank - start), 1.0, gram)
         tiles = [grown[8 * v : 8 * (v + 1), :] for v in range(rank // 8)]
-        return split(jnp.concatenate(eliminated(tiles, zero_ref[...]), axis=0))
+        return jnp.concatenate(eliminated(tiles, zero_ref[...], start), axis=0)
 
     weights = (a1_ref, a2_ref, a3_ref)
 
-    def iteration(turn, carry):
-        product, gram = carry
-        sized = split(full_product(factor_of(gram), under(split(product))))
-        second = factor_of(full_product(sized, over(sized), 1))
-        for at, part in enumerate(sized):
-            sized_ref[at] = part
-        for at, part in enumerate(second):
-            second_ref[at] = part
+    def iteration(turn, subspace):
+        sized = split(subspace)
         ahead = split(full_product(sized, [w[...] for w in weights]))
-        square = split(full_product(ahead, under(ahead), 1))
-        product = full_product(second, under(ahead))
-        half = full_product(second, under(square))
-        return product, full_product(split(half), over(second), 1)
-
-    product = full_product(split(start_ref[...]), [w[...] for w in weights])
-    parts = split(product)
-    lax.fori_loop(0, ITERS, iteration, (product, full_product(parts, over(parts), 1)))
-    subspace = full_product(
-        [second_ref[at] for at in range(3)], under([sized_ref[at] for at in range(3)])
-    )
+        square = full_product(ahead, under(ahead), 1)
+        gram = full_product(sized, over(sized), 1)
+        first = factor_of(square, rank)
+        second = factor_of(jnp.where(turn > 0, gram, jnp.where(lane == line, 1.0, 0.0)))
+        product = full_product(split(second), under(ahead))
+        turned = split(jnp.where((lane < rank) & (lane >= line), second, 0.0))
+        both = full_product(split(first), over(turned), 1)
+        return full_product(split(both), over(split(product)))
+
+    subspace = lax.fori_loop(0, ITERS, iteration, start_ref[...])
+    sized = split(subspace)
+    gram = full_product(sized, over(sized), 1)
+    subspace = full_product(split(factor_of(gram)), under(sized))
     rows = kept_ref.shape[0]
     component = lax.broadcasted_iota(jnp.int32, subspace.shape, 0)
     band = (component >= low_ref[0]) & (component < high_ref[0])
@@ -310,8 +298,6 @@
         out_specs=pl.BlockSpec(memory_space=pltpu.VMEM),
         scratch_shapes=[pltpu.VMEM((512, 512), jnp.bfloat16)] * 3
         + [
-            pltpu.VMEM((3, 64, 512), jnp.bfloat16),
-            pltpu.VMEM((3, 64, 128), jnp.bfloat16),
             pltpu.VMEM((rows, columns), frames.dtype),
             pltpu.VMEM((8, 128), jnp.float32),
             pltpu.SemaphoreType.DMA((chunks,)),

time: 81.3 us -> 79.2 us (0.974)
  Pallas kernels: 34.5 us -> 32.4 us
    pallas_call x1, Pallas kernels: 23.8 us -> 21.7 us  [power_of(): pl.pallas_call(functools.partial(power_kernel, chunks), out_shape=jax.Sha...]
where the time goes in v4:
time: 79.2 us; the launch traced here: 79 us
  Pallas kernels  32.4 us (41%)
  starting transfers between devices  17.8 us (22%)
  blocking collectives  13.8 us (17%)
  waiting for transfers between devices  13.2 us (17%)
  between operations  1.49 us (2%)
    pallas_call x1, Pallas kernels, power_of(): pl.pallas_call(functools.partial(power_kernel, chunks), out_shape=jax.Sha...  21.7 us
    all_to_all x1, blocking collectives, exchanged(): return lax.all_to_all(tiles, axes, 0, 0, tiled=True)  13.8 us
    all_to_all x1, waiting for transfers between devices, exchanged(): return lax.all_to_all(tiles, axes, 0, 0, tiled=True)  13.2 us
    pallas_call x1, Pallas kernels, local_gram(): pl.pallas_call(functools.partial(gram_kernel, chunks), out_shape=pltpu.VM...  10.6 us
    all_to_all x1, starting transfers between devices, exchanged(): return lax.all_to_all(tiles, axes, 0, 0, tiled=True)  10.6 us
    ppermute x3, starting transfers between devices, tile_rates(): lax.ppermute(decay, 'tm', [(i, (i + k) % steps) for i in range(steps)])  4.59 us
    ppermute x1, starting transfers between devices, swapped(): return lax.ppermute(x, 'core', [(0, 1), (1, 0)])  2.62 us
  transfers between devices with their start and end apart: 5, of which 1 were waited for; matrix products, arithmetic and copies ran while one was open for 0% of the time, Pallas kernels for 13%

profile of v4, /device:TPU:1, one launch (start us, length us, event | category | flops | bytes accessed | tf_op | source)
XLA Modules:
  0.0 79.0 jit_solution(11778976555218999065)
XLA Ops:
  0.0 0.0 copy-start.1
  0.0 0.0 copy-start
  0.0 3.6 %collective-permute-start.2 = (f32[500]{0:T(512)}, f32[500]{0:T(512)S(1)}, u32[]{:S(2)}, u32[]{:S(2)}) collective-permute-start(f32[500]{0:T(512)} %bitcast.13), channel_id=1, source_target_pairs={{0,96},{32,0},{64,32},{96,64},{1,97},{33,1},{65,33},{97,65},{2,98}... | collective-permute-start | bytes 6008 | tf_op jit(solution)/shard_map/ppermute | solution.py:314
  3.6 0.3 collective-permute-start.1
  3.9 0.7 collective-permute-start
  4.6 10.6 %local_gram.1 = f32[64,2,8,128]{3,2,1,0:T(8,128)} custom-call(bf16[1,500,16384]{2,1,0:T(8,128)(2,1)} %frames_ref.3), custom_call_target="tpu_custom_call" | custom-call | flops 8192000000 | bytes 16384000 | tf_op jit(solution)/shard_map/local_gram/pallas_call | solution.py:60
  15.2 10.6 %all-to-all-start = ((f32[128,8,128]{2,1,0:T(8,128)}), f32[128,8,128]{2,1,0:T(8,128)S(1)}, u32[]{:S(2)}, u32[]{:S(2)}) async-start(f32[128,8,128]{2,1,0:T(8,128)} %bitcast.1), calls=%async_computation | async-start | bytes 1048576 | tf_op jit(solution)/shard_map/all_to_all | solution.py:351
  26.0 0.1 compare_or_fusion
  26.0 0.0 collective-permute-done.2
  26.0 0.0 collective-permute-done.1
  26.0 0.0 collective-permute-done
  26.1 0.0 copy-done.1
  26.1 0.1 constant_dynamic-slice_fusion.2
  26.2 0.1 select_select_fusion.rates_ref
  26.3 13.2 %all-to-all-done.parts_ref = f32[128,8,128]{2,1,0:T(8,128)S(1)} async-done(((f32[128,8,128]{2,1,0:T(8,128)}), f32[128,8,128]{2,1,0:T(8,128)S(1)}, u32[]{:S(2)}, u32[]{:S(2)}) %all-to-all-start) | async-done | bytes 524320 | tf_op jit(solution)/shard_map/all_to_all | solution.py:351
  39.4 0.1 chain.1
  39.5 13.8 %all_to_all.10 = f32[64,8,128]{2,1,0:T(8,128)S(1)} all-to-all(f32[64,8,128]{2,1,0:T(8,128)S(1)} %chain.1), channel_id=1, replica_groups=mesh['tm'=4,'chip'=16,'core'=2] {'tm','chip'}, dimensions={0} | all-to-all | bytes 524288 | tf_op jit(solution)/shard_map/all_to_all | solution.py:351
  53.3 2.6 %collective-permute-start.3 = (f32[64,8,128]{2,1,0:T(8,128)S(1)}, f32[64,8,128]{2,1,0:T(8,128)S(1)}, u32[]{:S(2)}, u32[]{:S(2)}) collective-permute-start(f32[64,8,128]{2,1,0:T(8,128)S(1)} %all_to_all.10), channel_id=1, source_target_pairs={{0,1},{1,0},{2,3},{3,2},{4,5},{5,4},{6,7},{7,6},{8,9},{9,8},{10,11... | collective-permute-start | bytes 786440 | tf_op jit(solution)/shard_map/ppermute | solution.py:347
  57.2 0.0 copy-done
  57.3 0.0 collective-permute-done.3
  57.3 21.7 %power.1 = f32[1,16384]{1,0:T(1,128)} custom-call(s32[1]{0:T(128)} %bitcast.core_ref, f32[512,128]{1,0:T(8,128)S(1)} %bitcast.10, f32[512,128]{1,0:T(8,128)S(1)} %bitcast.11, f32[64,512]{1,0:T(8,128)S(1)} %pad.9.start_ref, s32[1]{0:T(128)S(6)} %copy.6.low_ref, s32[1]{0:T(128)S(6)} %copy.7.high_ref, bf16[1,500,16384]{2,1,0:T(8,128)(2,1)} %frames_ref.3), custom_call_target="tpu_custom_call" | custom-call | tf_op jit(solution)/shard_map/power/pallas_call | solution.py:286
  (9 shorter events, 0.1 us)
Async XLA Ops:
  0.0 26.1 %copy-start.1 = (f32[1,500]{1,0:T(1,128)S(1)}, f32[1,500]{1,0:T(1,128)}, u32[]{:S(2)}) copy-start(f32[1,500]{1,0:T(1,128)} %param.6) | copy-start | bytes 6004
  0.0 57.2 %copy-start = (f32[500,64]{0,1:T(8,128)S(1)}, f32[500,64]{0,1:T(8,128)}, u32[]{:S(2)}) copy-start(f32[500,64]{0,1:T(8,128)} %param.7) | copy-start | bytes 384004
  0.0 26.0 %collective-permute-start.2 = (f32[500]{0:T(512)}, f32[500]{0:T(512)S(1)}, u32[]{:S(2)}, u32[]{:S(2)}) collective-permute-start(f32[500]{0:T(512)} %bitcast.13), channel_id=1, source_target_pairs={{0,96},{32,0},{64,32},{96,64},{1,97},{33,1},{65,33},{97,65},{2,98}... | collective-permute-start | bytes 6008 | tf_op jit(solution)/shard_map/ppermute | solution.py:314
  3.6 22.5 %collective-permute-start.1 = (f32[500]{0:T(512)}, f32[500]{0:T(512)S(1)}, u32[]{:S(2)}, u32[]{:S(2)}) collective-permute-start(f32[500]{0:T(512)} %bitcast.14), channel_id=1, source_target_pairs={{0,64},{32,96},{64,0},{96,32},{1,65},{33,97},{65,1},{97,33},{2,66}... | collective-permute-start | bytes 6008 | tf_op jit(solution)/shard_map/ppermute | solution.py:314
  3.9 22.1 %collective-permute-start = (f32[500]{0:T(512)}, f32[500]{0:T(512)S(1)}, u32[]{:S(2)}, u32[]{:S(2)}) collective-permute-start(f32[500]{0:T(512)} %bitcast.15), channel_id=1, source_target_pairs={{0,32},{32,64},{64,96},{96,0},{1,33},{33,65},{65,97},{97,1},{2,34}... | collective-permute-start | bytes 6008 | tf_op jit(solution)/shard_map/ppermute | solution.py:314
  15.2 24.2 %all-to-all-start = ((f32[128,8,128]{2,1,0:T(8,128)}), f32[128,8,128]{2,1,0:T(8,128)S(1)}, u32[]{:S(2)}, u32[]{:S(2)}) async-start(f32[128,8,128]{2,1,0:T(8,128)} %bitcast.1), calls=%async_computation | async-start | bytes 1048576 | tf_op jit(solution)/shard_map/all_to_all | solution.py:351
  53.3 4.0 %collective-permute-start.3 = (f32[64,8,128]{2,1,0:T(8,128)S(1)}, f32[64,8,128]{2,1,0:T(8,128)S(1)}, u32[]{:S(2)}, u32[]{:S(2)}) collective-permute-start(f32[64,8,128]{2,1,0:T(8,128)S(1)} %all_to_all.10), channel_id=1, source_target_pairs={{0,1},{1,0},{2,3},{3,2},{4,5},{5,4},{6,7},{7,6},{8,9},{9,8},{10,11... | collective-permute-start | bytes 786440 | tf_op jit(solution)/shard_map/ppermute | solution.py:347
